TPU v7x, 512 devices: a whole 4x4x16 slice. The times are simulated.
512 devices in a mesh: node: 128 (over z, x, core), chan: 4 (over y).
Axes of the slice: x: 4, y: 4, z: 16, core: 2. Of those that a mesh axis runs over, the one named last changes fastest.
Arguments:
- nodes: bfloat16 [16384, 512], P('node'), may hold values from -6 to 6
- edges: bfloat16 [49152, 512], P('node'), may hold values from -6 to 6
- grad_nodes_in: bfloat16 [16384, 512], P('node'), may hold values from -6 to 6
- grad_edges_in: bfloat16 [49152, 512], P('node'), may hold values from -6 to 6
- edge_in_weight: bfloat16 [1536, 512], P(None, 'chan'), may hold values from -0.15625 to 0.15625
- edge_bias: float32 [512], P('chan'), may hold values from -4 to 4
- edge_out_weight: bfloat16 [512, 512], P('chan'), may hold values from -0.25 to 0.25
- node_in_weight: bfloat16 [1024, 512], P(None, 'chan'), may hold values from -0.1875 to 0.1875
- node_bias: float32 [512], P('chan'), may hold values from -4 to 4
- node_out_weight: bfloat16 [512, 512], P('chan'), may hold values from -0.25 to 0.25
- senders: int32 [49152], P('node'), may hold values from 0 to 255
- receivers: int32 [49152], P('node'), may hold values from 0 to 127, as said below
- valid_counts: int32 [384], P('node'), may hold values from 1 to 128
- send_list: int32 [16384, 1], P('node'), may hold values from 0 to 127
Outputs:
- grad_nodes: bfloat16 [16384, 512], P('node', 'chan')
- grad_edges: bfloat16 [49152, 512], P('node', 'chan')
- grad_edge_in: float32 [1536, 512], P('node', 'chan')
- grad_edge_out: float32 [512, 512], P('chan', 'node')
- grad_node_in: float32 [1024, 512], P('node', 'chan')
- grad_node_out: float32 [512, 512], P('chan', 'node')
Inputs may be any that keep to these rules, and one draw needn't show every extreme that they name: `senders`: below 128: a node of the slot's own owner; otherwise 128 + p + j, the j-th node that owner p sends to the slot's owner. `receivers`: A node number on the slot's owner, nondecreasing within each owner's 384 slots. `valid_counts`: the live slots of a block are its first ones. `send_list`: row p * 128 + q holds node numbers of owner p that owner q reads.
All inputs are finite; a program needn't handle non-finite values.
Results may differ from a plain program's by a relative error of at most 0.011.
Values may be sent and summed in bfloat16 or wider, within the bound.
A program may use at most 64 MiB of HBM per device.

v0:
```python
import jax
import jax.numpy as jnp
from jax import lax
from jax.sharding import Mesh
from jax.sharding import PartitionSpec as P

NODE = ("node_0", "node_1", "node_2")


def sent_to_all(shard, axis):
    count = lax.axis_size(axis)
    return lax.all_to_all(
        jnp.broadcast_to(shard[None], (count, *shard.shape)), axis, 0, 0, tiled=True
    )


def taken_together(shard, axis):
    everything = sent_to_all(shard, axis)
    return jnp.sum(everything, axis=0)


def over_copies(shard, axis):
    return sent_to_all(shard, axis).astype(jnp.float32).sum(axis=0)


def laid_out(pieces, dim):
    pieces = jnp.moveaxis(pieces, 0, dim)
    shape = pieces.shape
    return pieces.reshape(*shape[:dim], shape[dim] * shape[dim + 1], *shape[dim + 2 :])


def collect(shard, axis, dim):
    pieces = sent_to_all(shard, axis)
    return laid_out(pieces, dim)


def split_up(shard, dim, count):
    before, after = (shard.shape[:dim], shard.shape[dim + 1 :])
    return jnp.moveaxis(shard.reshape(*before, count, -1, *after), dim, 0)


def sum_at_owner(shard, axis, dim):
    pieces = split_up(shard, dim, lax.axis_size(axis))
    arrived = lax.all_to_all(pieces, axis, split_axis=0, concat_axis=0, tiled=True)
    return arrived.astype(jnp.float32).sum(axis=0)


def summed_rows(shard, axes, dim):
    far, near = axes
    pieces = split_up(shard, dim, lax.axis_size(far))
    nearer = sum_at_owner(pieces, near, dim + 1)
    arrived = lax.all_to_all(
        nearer.astype(jnp.bfloat16), far, split_axis=0, concat_axis=0, tiled=True
    )
    return arrived.astype(jnp.float32).sum(axis=0)


def side_by_side(arrays, axis, dim, along):
    both = jnp.concatenate(arrays, axis=along)
    filled, at, outs = (summed_rows(both, axis, dim), 0, [])
    for a in arrays:
        outs.append(lax.slice_in_dim(filled, at, at + a.shape[along], axis=along))
        at += a.shape[along]
    return tuple(outs)


def silu_parts(preact):
    logistic = jax.nn.sigmoid(preact)
    return (preact * logistic, logistic * (1.0 + preact * (1.0 - logistic)))


def contract(left_mat, right_mat, left_dim, right_dim):
    return lax.dot_general(
        left_mat,
        right_mat,
        (((left_dim,), (right_dim,)), ((), ())),
        preferred_element_type=jnp.float32,
    )


def seg_total(values, ids, count):
    return jax.ops.segment_sum(values, ids, num_segments=count)


def body(
    nodes,
    edges,
    grad_nodes_in,
    grad_edges_in,
    edge_in_weight,
    edge_bias,
    edge_out_weight,
    node_in_weight,
    node_bias,
    node_out_weight,
    senders,
    receivers,
    valid_counts,
    send_list,
):
    local_count = nodes.shape[0]
    edge_count = edges.shape[0]
    feat_width = nodes.shape[1]
    edge_block = edge_count // valid_counts.shape[0]
    col_share = feat_width // lax.axis_size("chan")
    col_start = lax.axis_index("chan") * col_share
    wanted = send_list.reshape(-1)
    outgoing = nodes[wanted]
    halo_feats = lax.all_to_all(outgoing, NODE, split_axis=0, concat_axis=0, tiled=True)
    node_table = jnp.concatenate([nodes, halo_feats], axis=0)
    table_count = node_table.shape[0]
    stacked = jnp.concatenate([edges, node_table[senders], nodes[receivers]], axis=1)
    position = lax.broadcasted_iota(jnp.int32, (edge_count,), 0) % edge_block
    live_mask = (position < jnp.repeat(valid_counts, edge_block)).astype(jnp.float32)[:, None]
    recv_onehot = receivers[:, None] == lax.broadcasted_iota(jnp.int32, (1, local_count), 1)
    edge_pre = jnp.dot(stacked, edge_in_weight, preferred_element_type=jnp.float32) + edge_bias
    edge_act, edge_slope = silu_parts(edge_pre)
    hidden = (edge_act * live_mask).astype(jnp.bfloat16)
    hidden_sums = contract(recv_onehot.astype(jnp.bfloat16), hidden, 0, 0).astype(jnp.bfloat16)
    agg_terms = jnp.dot(hidden_sums, edge_out_weight, preferred_element_type=jnp.float32)
    aggregate = taken_together(agg_terms, "chan").astype(jnp.bfloat16)
    node_cat = jnp.concatenate([nodes, aggregate], axis=1)
    node_pre = jnp.dot(node_cat, node_in_weight, preferred_element_type=jnp.float32) + node_bias
    node_act, node_slope = silu_parts(node_pre)
    node_hidden = node_act.astype(jnp.bfloat16)
    node_pre_grad = (contract(grad_nodes_in, node_out_weight, 1, 1) * node_slope).astype(
        jnp.bfloat16
    )
    grad_node_out = contract(node_hidden, grad_nodes_in, 0, 0)
    grad_node_in = contract(node_cat, node_pre_grad, 0, 0)
    node_back = contract(node_pre_grad, node_in_weight, 1, 1)
    node_full = over_copies(node_back.astype(jnp.bfloat16), "chan").astype(jnp.float32)
    grad_aggregate = node_full[:, feat_width:]
    message_grad = (grad_edges_in.astype(jnp.float32) + grad_aggregate[receivers]).astype(
        jnp.bfloat16
    )
    edge_pre_grad = (contract(message_grad, edge_out_weight, 1, 1) * edge_slope * live_mask).astype(
        jnp.bfloat16
    )
    grad_edge_out = contract(hidden, message_grad, 0, 0)
    grad_edge_in = contract(stacked, edge_pre_grad, 0, 0)
    own_nodes = lax.dynamic_slice_in_dim(grad_nodes_in, col_start, col_share, 1).astype(jnp.float32)
    own_edges = lax.dynamic_slice_in_dim(grad_edges_in, col_start, col_share, 1).astype(jnp.float32)
    hidden_share = edge_in_weight.shape[1]
    blocks = edge_in_weight.reshape(3, feat_width, hidden_share)
    full_grad = collect(edge_pre_grad, "chan", 1)
    share_rows = lax.all_to_all(blocks, "chan", split_axis=1, concat_axis=2, tiled=True)
    full_rows = share_rows.reshape(3 * col_share, share_rows.shape[2])
    edge_own = contract(full_grad, full_rows, 1, 1)
    sender_terms = seg_total(edge_own[:, col_share : 2 * col_share], senders, table_count)
    receiver_terms = seg_total(edge_own[:, 2 * col_share :], receivers, local_count)
    node_own = lax.dynamic_slice_in_dim(node_full, col_start, col_share, 1)
    returned = lax.all_to_all(
        sender_terms[local_count:].astype(jnp.bfloat16),
        NODE,
        split_axis=0,
        concat_axis=0,
        tiled=True,
    ).astype(jnp.float32)
    node_total = (
        sender_terms[:local_count]
        + receiver_terms
        + node_own
        + seg_total(returned, wanted, local_count)
    )
    summed_edges = edge_own[:, :col_share]
    grad_nodes = (own_nodes + node_total).astype(jnp.bfloat16)
    grad_edges = (own_edges + summed_edges).astype(jnp.bfloat16)
    rows_edge, rows_node = (
        summed_rows(grad_edge_in.astype(jnp.bfloat16), (("node_0", "node_1"), "node_2"), 0),
        summed_rows(grad_node_in.astype(jnp.bfloat16), (("node_0", "node_1"), "node_2"), 0),
    )
    cols_edge, cols_node = side_by_side(
        (grad_edge_out.astype(jnp.bfloat16), grad_node_out.astype(jnp.bfloat16)),
        (("node_0", "node_1"), "node_2"),
        1,
        0,
    )
    return (grad_nodes, grad_edges, rows_edge, cols_edge, rows_node, cols_node)


def solution(mesh):
    split = Mesh(
        mesh.devices.reshape(16, 4, 2, mesh.shape["chan"]), ("node_0", "node_1", "node_2", "chan")
    )
    in_specs = (
        P(NODE, None),
        P(NODE, None),
        P(NODE, None),
        P(NODE, None),
        P(None, "chan"),
        P("chan"),
        P("chan", None),
        P(None, "chan"),
        P("chan"),
        P("chan", None),
        P(NODE),
        P(NODE),
        P(NODE),
        P(NODE, None),
    )
    out_specs = (
        P(NODE, "chan"),
        P(NODE, "chan"),
        P(NODE, "chan"),
        P("chan", NODE),
        P(NODE, "chan"),
        P("chan", NODE),
    )
    return jax.shard_map(body, mesh=split, in_specs=in_specs, out_specs=out_specs, check_vma=False)
```

profile of v0, /device:TPU:1, one launch (start us, length us, event | category | flops | bytes accessed | tf_op | source)
XLA Modules:
  0.0 215.5 jit_solution(5181485937799210386)
XLA Ops:
  1.4 1.8 gather_fusion
  5.1 20.4 %all-to-all-start = ((bf16[128,2,256]{2,1,0:T(2,128)(2,1)}), bf16[128,2,256]{2,1,0:T(2,128)(2,1)S(1)}, u32[]{:S(2)}, u32[]{:S(2)}) async-start(bf16[128,2,256]{2,1,0:T(2,128)(2,1)} %reshape.133), calls=%async_computation | async-start | bytes 262144 | tf_op jit(solution)/shard_map/all_to_all | solution.py:109
  25.5 2.1 gather_fusion.2
  27.7 13.7 %all-to-all-done = bf16[128,2,256]{2,1,0:T(2,128)(2,1)S(1)} async-done(((bf16[128,2,256]{2,1,0:T(2,128)(2,1)}), bf16[128,2,256]{2,1,0:T(2,128)(2,1)S(1)}, u32[]{:S(2)}, u32[]{:S(2)}) %all-to-all-start) | async-done | bytes 131104 | tf_op jit(solution)/shard_map/all_to_all | solution.py:109
  41.6 2.1 gather_fusion.1
  46.8 4.2 %all-to-all-start.1 = ((f32[4,128,512]{2,1,0:T(8,128)}), f32[4,128,512]{2,1,0:T(8,128)S(1)}, u32[]{:S(2)}, u32[]{:S(2)}) async-start(f32[4,128,512]{2,1,0:T(8,128)} %broadcast_in_dim.23), calls=%async_computation.1 | async-start | bytes 2097152 | tf_op jit(solution)/shard_map/all_to_all | solution.py:12
  52.1 13.4 %all-to-all-done.1 = f32[4,128,512]{2,1,0:T(8,128)S(1)} async-done(((f32[4,128,512]{2,1,0:T(8,128)}), f32[4,128,512]{2,1,0:T(8,128)S(1)}, u32[]{:S(2)}, u32[]{:S(2)}) %all-to-all-start.1) | async-done | bytes 1048608 | tf_op jit(solution)/shard_map/all_to_all | solution.py:12
  65.5 3.5 %all-to-all-start.4 = ((bf16[3,512,128]{2,0,1:T(4,128)(2,1)}), bf16[3,512,128]{2,0,1:T(4,128)(2,1)S(1)}, u32[]{:S(2)}, u32[]{:S(2)}) async-start(bf16[3,512,128]{2,0,1:T(4,128)(2,1)} %copy.77), calls=%async_computation.4 | async-start | bytes 1048576 | tf_op jit(solution)/shard_map/all_to_all | solution.py:147
  70.8 6.0 %all-to-all-done.4 = bf16[3,512,128]{2,0,1:T(4,128)(2,1)S(1)} async-done(((bf16[3,512,128]{2,0,1:T(4,128)(2,1)}), bf16[3,512,128]{2,0,1:T(4,128)(2,1)S(1)}, u32[]{:S(2)}, u32[]{:S(2)}) %all-to-all-start.4) | async-done | bytes 393248 | tf_op jit(solution)/shard_map/all_to_all | solution.py:147
  76.7 6.2 %all_to_all.81 = bf16[2,64,8,128]{3,2,1,0:T(8,128)(2,1)S(1)} all-to-all(bf16[2,64,8,128]{3,2,1,0:T(8,128)(2,1)S(1)} %bitcast.62), channel_id=1, replica_groups=mesh['node_0'=16,'node_1'=4,'node_2'=2,'chan'=4] {'node_2'}, dimensions={0} | all-to-all | bytes 524288 | tf_op jit(solution)/shard_map/all_to_all | solution.py:44
  84.1 3.5 %all-to-all-start.2 = ((bf16[4,128,1024]{2,1,0:T(8,128)(2,1)}), bf16[4,128,1024]{2,1,0:T(8,128)(2,1)S(1)}, u32[]{:S(2)}, u32[]{:S(2)}) async-start(bf16[4,128,1024]{2,1,0:T(8,128)(2,1)} %broadcast_in_dim.48), calls=%async_computation.2 | async-start | bytes 2097152 | tf_op jit(solution)/shard_map/all_to_all | solution.py:12
  89.6 12.8 %all-to-all-done.2 = bf16[4,128,1024]{2,1,0:T(8,128)(2,1)S(1)} async-done(((bf16[4,128,1024]{2,1,0:T(8,128)(2,1)}), bf16[4,128,1024]{2,1,0:T(8,128)(2,1)S(1)}, u32[]{:S(2)}, u32[]{:S(2)}) %all-to-all-start.2) | async-done | bytes 1048608 | tf_op jit(solution)/shard_map/all_to_all | solution.py:12
  103.4 1.6 gather_fusion.3
  105.0 1.2 fusion.1
  107.2 3.5 %all-to-all-start.3 = ((bf16[4,384,128]{1,2,0:T(8,128)(2,1)}), bf16[4,384,128]{1,2,0:T(8,128)(2,1)S(1)}, u32[]{:S(2)}, u32[]{:S(2)}) async-start(bf16[4,384,128]{1,2,0:T(8,128)(2,1)} %broadcast_in_dim.49), calls=%async_computation.3 | async-start | bytes 786432 | tf_op jit(solution)/shard_map/all_to_all | solution.py:12
  110.6 1.3 convolution_convert_fusion.3
  112.5 4.8 %all-to-all-done.3 = bf16[4,384,128]{1,2,0:T(8,128)(2,1)S(1)} async-done(((bf16[4,384,128]{1,2,0:T(8,128)(2,1)}), bf16[4,384,128]{1,2,0:T(8,128)(2,1)S(1)}, u32[]{:S(2)}, u32[]{:S(2)}) %all-to-all-start.3) | async-done | bytes 393248 | tf_op jit(solution)/shard_map/all_to_all | solution.py:12
  117.2 6.2 %all-to-all-start.11 = ((bf16[64,8,128]{2,1,0:T(8,128)(2,1)}), bf16[64,8,128]{2,1,0:T(8,128)(2,1)S(1)}, u32[]{:S(2)}, u32[]{:S(2)}) async-start(bf16[64,8,128]{2,1,0:T(8,128)(2,1)} %reduce_sum.87), calls=%async_computation.11 | async-start | bytes 262144 | tf_op jit(solution)/shard_map/all_to_all | solution.py:52
  124.4 1.9 scatter_custom_fusion
  127.0 11.3 %all-to-all-done.11 = bf16[64,8,128]{2,1,0:T(8,128)(2,1)S(1)} async-done(((bf16[64,8,128]{2,1,0:T(8,128)(2,1)}), bf16[64,8,128]{2,1,0:T(8,128)(2,1)S(1)}, u32[]{:S(2)}, u32[]{:S(2)}) %all-to-all-start.11) | async-done | bytes 131104 | tf_op jit(solution)/shard_map/all_to_all | solution.py:52
  138.3 7.5 %all_to_all.82 = bf16[2,64,256,4]{2,1,3,0:T(8,128)(2,1)S(1)} all-to-all(bf16[2,64,256,4]{2,1,3,0:T(8,128)(2,1)S(1)} %bitcast.61), channel_id=1, replica_groups=mesh['node_0'=16,'node_1'=4,'node_2'=2,'chan'=4] {'node_2'}, dimensions={0} | all-to-all | bytes 524288 | tf_op jit(solution)/shard_map/all_to_all | solution.py:44
  145.8 4.0 %all_to_all.83 = bf16[2,64,12,128]{3,1,2,0:T(8,128)(2,1)S(1)} all-to-all(bf16[2,64,12,128]{3,1,2,0:T(8,128)(2,1)S(1)} %copy.82), channel_id=1, replica_groups=mesh['node_0'=16,'node_1'=4,'node_2'=2,'chan'=4] {'node_2'}, dimensions={0} | all-to-all | bytes 786432 | tf_op jit(solution)/shard_map/all_to_all | solution.py:44
  149.8 5.5 %all-to-all-start.5 = ((bf16[128,1,128]{2,1,0:T(2,128)(2,1)}), bf16[128,1,128]{2,1,0:T(2,128)(2,1)S(1)}, u32[]{:S(2)}, u32[]{:S(2)}) async-start(bf16[128,1,128]{2,1,0:T(2,128)(2,1)} %copy.80), calls=%async_computation.5 | async-start | bytes 131072 | tf_op jit(solution)/shard_map/all_to_all | solution.py:153
  156.2 14.2 %all-to-all-done.5 = bf16[128,1,128]{2,1,0:T(2,128)(2,1)S(1)} async-done(((bf16[128,1,128]{2,1,0:T(2,128)(2,1)}), bf16[128,1,128]{2,1,0:T(2,128)(2,1)S(1)}, u32[]{:S(2)}, u32[]{:S(2)}) %all-to-all-start.5) | async-done | bytes 32800 | tf_op jit(solution)/shard_map/all_to_all | solution.py:153
  170.4 4.6 %all-to-all-start.9 = ((bf16[64,256,4]{1,2,0:T(4,128)(2,1)}), bf16[64,256,4]{1,2,0:T(4,128)(2,1)S(1)}, u32[]{:S(2)}, u32[]{:S(2)}) async-start(bf16[64,256,4]{1,2,0:T(4,128)(2,1)} %copy.86), calls=%async_computation.9 | async-start | bytes 262144 | tf_op jit(solution)/shard_map/all_to_all | solution.py:52
  177.4 2.7 %scatter_custom_fusion.1 = f32[128,128]{1,0:T(8,128)S(1)} fusion(f32[128,128]{1,0:T(8,128)S(1)} %slice_add_fusion.1, s32[384]{0:T(512)S(1)} %copy-done.14, f32[384,384]{1,0:T(8,128)S(1)} %fusion.4), kind=kCustom, calls=%fused_computation.35 | custom fusion | flops 49152 | bytes 262144 | tf_op jit(solution)/shard_map/scatter-add | solution.py:82
  180.2 10.6 %all-to-all-done.9 = bf16[64,256,4]{1,2,0:T(4,128)(2,1)S(1)} async-done(((bf16[64,256,4]{1,2,0:T(4,128)(2,1)}), bf16[64,256,4]{1,2,0:T(4,128)(2,1)S(1)}, u32[]{:S(2)}, u32[]{:S(2)}) %all-to-all-start.9) | async-done | bytes 131104 | tf_op jit(solution)/shard_map/all_to_all | solution.py:52
  190.8 5.7 %all-to-all-start.7 = ((bf16[64,12,128]{2,1,0:T(8,128)(2,1)}), bf16[64,12,128]{2,1,0:T(8,128)(2,1)S(1)}, u32[]{:S(2)}, u32[]{:S(2)}) async-start(bf16[64,12,128]{2,1,0:T(8,128)(2,1)} %copy.83), calls=%async_computation.7 | async-start | bytes 524288 | tf_op jit(solution)/shard_map/all_to_all | solution.py:52
  196.5 1.6 fusion.7
  198.0 1.2 scatter_custom_fusion.2
  199.2 1.4 add_convert_fusion.1
  201.3 13.6 %all-to-all-done.7 = bf16[64,12,128]{2,1,0:T(8,128)(2,1)S(1)} async-done(((bf16[64,12,128]{2,1,0:T(8,128)(2,1)}), bf16[64,12,128]{2,1,0:T(8,128)(2,1)S(1)}, u32[]{:S(2)}, u32[]{:S(2)}) %all-to-all-start.7) | async-done | bytes 196640 | tf_op jit(solution)/shard_map/all_to_all | solution.py:52
  (90 shorter events, 20.3 us)
Async XLA Ops:
  0.6 68.5 %copy-start = (bf16[1024,128]{1,0:T(8,128)(2,1)S(1)}, bf16[1024,128]{1,0:T(8,128)(2,1)}, u32[]{:S(2)}) copy-start(bf16[1024,128]{1,0:T(8,128)(2,1)} %param.21) | copy-start | bytes 786436
  0.6 24.9 %copy-start.1 = (bf16[128,512]{1,0:T(8,128)(2,1)S(1)}, bf16[128,512]{1,0:T(8,128)(2,1)}, u32[]{:S(2)}) copy-start(bf16[128,512]{1,0:T(8,128)(2,1)} %param.14) | copy-start | bytes 393220
  0.7 24.8 %copy-start.13 = (s32[384]{0:T(512)S(1)}, s32[384]{0:T(512)}, u32[]{:S(2)}) copy-start(s32[384]{0:T(512)} %param.24) | copy-start | bytes 4612
  0.7 24.8 %copy-start.14 = (s32[384]{0:T(512)S(1)}, s32[384]{0:T(512)}, u32[]{:S(2)}) copy-start(s32[384]{0:T(512)} %param.25) | copy-start | bytes 4612
  5.1 36.4 %all-to-all-start = ((bf16[128,2,256]{2,1,0:T(2,128)(2,1)}), bf16[128,2,256]{2,1,0:T(2,128)(2,1)S(1)}, u32[]{:S(2)}, u32[]{:S(2)}) async-start(bf16[128,2,256]{2,1,0:T(2,128)(2,1)} %reshape.133), calls=%async_computation | async-start | bytes 262144 | tf_op jit(solution)/shard_map/all_to_all | solution.py:109
  25.5 2.1 copy-start.8
  25.5 2.1 copy-start.15
  43.7 1.0 copy-start.2
  43.7 1.0 copy-start.16
  43.8 1.4 copy-start.18
  45.2 1.6 copy-start.4
  46.8 18.7 %all-to-all-start.1 = ((f32[4,128,512]{2,1,0:T(8,128)}), f32[4,128,512]{2,1,0:T(8,128)S(1)}, u32[]{:S(2)}, u32[]{:S(2)}) async-start(f32[4,128,512]{2,1,0:T(8,128)} %broadcast_in_dim.23), calls=%async_computation.1 | async-start | bytes 2097152 | tf_op jit(solution)/shard_map/all_to_all | solution.py:12
  65.5 11.2 %all-to-all-start.4 = ((bf16[3,512,128]{2,0,1:T(4,128)(2,1)}), bf16[3,512,128]{2,0,1:T(4,128)(2,1)S(1)}, u32[]{:S(2)}, u32[]{:S(2)}) async-start(bf16[3,512,128]{2,0,1:T(4,128)(2,1)} %copy.77), calls=%async_computation.4 | async-start | bytes 1048576 | tf_op jit(solution)/shard_map/all_to_all | solution.py:147
  69.0 1.0 copy-start.9
  69.0 1.0 copy-start.17
  70.0 12.9 %copy-start.11 = (f32[128,128]{1,0:T(8,128)}, f32[128,128]{1,0:T(8,128)S(1)}, u32[]{:S(2)}) copy-start(f32[128,128]{1,0:T(8,128)S(1)} %convolution_add_fusion.1) | copy-start | bytes 196612
  84.1 18.3 %all-to-all-start.2 = ((bf16[4,128,1024]{2,1,0:T(8,128)(2,1)}), bf16[4,128,1024]{2,1,0:T(8,128)(2,1)S(1)}, u32[]{:S(2)}, u32[]{:S(2)}) async-start(bf16[4,128,1024]{2,1,0:T(8,128)(2,1)} %broadcast_in_dim.48), calls=%async_computation.2 | async-start | bytes 2097152 | tf_op jit(solution)/shard_map/all_to_all | solution.py:12
  87.6 1.1 copy-start.10
  87.7 1.0 copy-start.12
  102.6 0.8 copy-start.3
  103.4 1.7 copy-start.5
  103.4 1.7 copy-start.6
  107.2 10.1 %all-to-all-start.3 = ((bf16[4,384,128]{1,2,0:T(8,128)(2,1)}), bf16[4,384,128]{1,2,0:T(8,128)(2,1)S(1)}, u32[]{:S(2)}, u32[]{:S(2)}) async-start(bf16[4,384,128]{1,2,0:T(8,128)(2,1)} %broadcast_in_dim.49), calls=%async_computation.3 | async-start | bytes 786432 | tf_op jit(solution)/shard_map/all_to_all | solution.py:12
  112.0 11.5 %copy-start.7 = (bf16[128,512]{1,0:T(8,128)(2,1)S(1)}, bf16[128,512]{1,0:T(8,128)(2,1)}, u32[]{:S(2)}) copy-start(bf16[128,512]{1,0:T(8,128)(2,1)} %convolution_convert_fusion.4) | copy-start | bytes 393220
  117.2 21.1 %all-to-all-start.11 = ((bf16[64,8,128]{2,1,0:T(8,128)(2,1)}), bf16[64,8,128]{2,1,0:T(8,128)(2,1)S(1)}, u32[]{:S(2)}, u32[]{:S(2)}) async-start(bf16[64,8,128]{2,1,0:T(8,128)(2,1)} %reduce_sum.87), calls=%async_computation.11 | async-start | bytes 262144 | tf_op jit(solution)/shard_map/all_to_all | solution.py:52
  149.8 20.6 %all-to-all-start.5 = ((bf16[128,1,128]{2,1,0:T(2,128)(2,1)}), bf16[128,1,128]{2,1,0:T(2,128)(2,1)S(1)}, u32[]{:S(2)}, u32[]{:S(2)}) async-start(bf16[128,1,128]{2,1,0:T(2,128)(2,1)} %copy.80), calls=%async_computation.5 | async-start | bytes 131072 | tf_op jit(solution)/shard_map/all_to_all | solution.py:153
  170.4 20.4 %all-to-all-start.9 = ((bf16[64,256,4]{1,2,0:T(4,128)(2,1)}), bf16[64,256,4]{1,2,0:T(4,128)(2,1)S(1)}, u32[]{:S(2)}, u32[]{:S(2)}) async-start(bf16[64,256,4]{1,2,0:T(4,128)(2,1)} %copy.86), calls=%async_computation.9 | async-start | bytes 262144 | tf_op jit(solution)/shard_map/all_to_all | solution.py:52
  190.8 24.0 %all-to-all-start.7 = ((bf16[64,12,128]{2,1,0:T(8,128)(2,1)}), bf16[64,12,128]{2,1,0:T(8,128)(2,1)S(1)}, u32[]{:S(2)}, u32[]{:S(2)}) async-start(bf16[64,12,128]{2,1,0:T(8,128)(2,1)} %copy.83), calls=%async_computation.7 | async-start | bytes 524288 | tf_op jit(solution)/shard_map/all_to_all | solution.py:52
where the time goes:
time: 219 us; the launch traced here: 215 us
  waiting for transfers between devices  100 us (46%)
  starting transfers between devices  57 us (26%)
  local copies, waits for them, and re-layouts  18.7 us (9%)
  blocking collectives  17.8 us (8%)
  other arithmetic  13.6 us (6%)
  matrix products  6.81 us (3%)
    all_to_all x3, waiting for transfers between devices, summed_rows(): lax.all_to_all(nearer.astype(jnp.bfloat16), far, split_axis=0, concat_axi...  35.5 us
    all_to_all x3, waiting for transfers between devices, sent_to_all(): lax.all_to_all(jnp.broadcast_to(shard[None], (count, *shard.shape)), axis...  31 us
    all_to_all x1, starting transfers between devices, body(): lax.all_to_all(outgoing, NODE, split_axis=0, concat_axis=0, tiled=True)  20.4 us
    all_to_all x3, blocking collectives, sum_at_owner(): lax.all_to_all(pieces, axis, split_axis=0, concat_axis=0, tiled=True)  17.8 us
    all_to_all x3, starting transfers between devices, summed_rows(): lax.all_to_all(nearer.astype(jnp.bfloat16), far, split_axis=0, concat_axi...  16.5 us
    all_to_all x1, waiting for transfers between devices, body(): lax.all_to_all(sender_terms[local_count:].astype(jnp.bfloat16), NODE, spl...  14.2 us
    all_to_all x1, waiting for transfers between devices, body(): lax.all_to_all(outgoing, NODE, split_axis=0, concat_axis=0, tiled=True)  13.7 us
    all_to_all x3, starting transfers between devices, sent_to_all(): lax.all_to_all(jnp.broadcast_to(shard[None], (count, *shard.shape)), axis...  11.2 us
  transfers between devices with their start and end apart: 9, of which 9 were waited for; matrix products, arithmetic and copies ran while one was open for 11% of the time, Pallas kernels for 0%

commit v1 on v0

v1 whole, which is shorter than its diff:
```python
import functools

import jax
import jax.numpy as jnp
from jax import lax
from jax.experimental import pallas as pl
from jax.experimental.pallas import tpu as pltpu
from jax.sharding import Mesh
from jax.sharding import PartitionSpec as P

NODE = ("z", "x", "c")
MESH = pl.DeviceIdType.MESH
F32 = jnp.float32
BF16 = jnp.bfloat16


def dot(a, b):
    return jnp.dot(a, b, preferred_element_type=F32)


def dot_t(a, b):
    return lax.dot_general(a, b, (((1,), (1,)), ((), ())), preferred_element_type=F32)


def t_dot(a, b):
    return lax.dot_general(a, b, (((0,), (0,)), ((), ())), preferred_element_type=F32)


def iota(shape, dim):
    return lax.broadcasted_iota(jnp.int32, shape, dim)


def hot(cond):
    return jnp.where(cond, 1.0, 0.0).astype(BF16)


def two_parts(v):
    high = v.astype(BF16)
    return high, (v - high.astype(F32)).astype(BF16)


def sigmoid(v):
    return 1.0 / (1.0 + jnp.exp(-v))


def kernel(
    nz,
    nx,
    ny,
    sl_ref,
    snd_ref,
    rcv_ref,
    vc_ref,
    n_ref,
    e_ref,
    gn_ref,
    ge_ref,
    win_ref,
    be_ref,
    wout_ref,
    wn_ref,
    bn_ref,
    wno_ref,
    o_nodes,
    o_edges,
    o_ei,
    o_eo,
    o_ni,
    o_no,
    out1,
    r1,
    out2,
    r2,
    wout_g,
    wn2_g,
    rows_g,
    wn1_g,
    hs_b,
    hs_g,
    npg_b,
    npg_g,
    epg_b,
    epg_g,
    ga_f,
    gb_f,
    g1,
    g2,
    g3,
    g4,
    ha,
    hb,
    ca,
    cb,
    xa,
    xb,
    rxa,
    rxb,
    za,
    zb,
    rza,
    rzb,
    s_out,
    s_a,
    s_mid,
    s_b,
    send,
    recv,
):
    z, x, c, y = (lax.axis_index(a) for a in ("z", "x", "c", "y"))
    nxc = 2 * nx
    owners = nz * nxc
    nd, d_feat = n_ref.shape
    ed = e_ref.shape[0]
    hs_w = wout_ref.shape[0]
    fs_w = d_feat // ny
    block = ed // vc_ref.shape[0]

    def by(**kw):
        return kw

    z_off = lambda d: by(z=lax.rem(z + d, nz))
    y_off = lambda d: by(y=lax.rem(y + d, ny))
    xc_off = lambda k: by(x=lax.rem(x + k // 2, nx), c=c if k % 2 == 0 else 1 - c)
    xc_back = lambda k: by(x=lax.rem(x + nx - k // 2, nx), c=c if k % 2 == 0 else 1 - c)
    z_back = lambda d: by(z=lax.rem(z + nz - d, nz))

    barrier = pltpu.get_barrier_semaphore()
    peers = (
        [z_off(d) for d in range(1, nz)]
        + [xc_off(k) for k in range(1, nxc)]
        + [y_off(d) for d in range(1, ny)]
    )
    for peer in peers:
        pl.semaphore_signal(barrier, inc=1, device_id=peer, device_id_type=MESH)

    def push(phase, src, dst, peer):
        pltpu.make_async_remote_copy(
            src_ref=src,
            dst_ref=dst,
            send_sem=send.at[phase],
            recv_sem=recv.at[phase],
            device_id=peer,
            device_id_type=MESH,
        ).start()

    def arrived(phase, ref):
        pltpu.make_async_copy(ref, ref, recv.at[phase]).wait()

    def left(phase, ref):
        pltpu.make_async_copy(ref, ref, send.at[phase]).wait()

    nodes = n_ref[...]
    r_q = iota((owners, owners), 1)
    k_of, dz_of = r_q // nz, r_q % nz
    q_of = (
        ((z + dz_of) & (nz - 1)) * nxc
        + ((x + (k_of >> 1)) & (nx - 1)) * 2
        + (c ^ (k_of & 1))
    )
    perm_q = hot(iota((owners, owners), 0) == q_of)
    sl_hot = hot(iota((nd, owners), 0) == sl_ref[...])
    sl_perm = dot(sl_hot, perm_q).astype(BF16)
    rows_out = t_dot(sl_perm, nodes).astype(BF16)
    for k in range(nxc):
        out1[k] = rows_out[k * nz : (k + 1) * nz]
    r1[0] = rows_out[0:nz]

    pl.semaphore_wait(barrier, len(peers))

    for k in range(1, nxc):
        push(0, out1.at[k], r1.at[k], xc_off(k))
    for d in range(1, ny):
        push(2, wout_ref, wout_g.at[d - 1], y_off(d))
    for d in range(1, ny):
        push(3, wn_ref.at[1], wn2_g.at[d - 1], y_off(d))

    t_i = iota((owners, owners), 0)
    stage = hot(iota((owners, owners), 1) == (t_i % nxc) * nz + t_i // nxc)
    arrived(0, r1.at[pl.ds(1, nxc - 1)])
    second = dot(stage, r1[...].reshape(owners, d_feat)).astype(BF16)
    for d in range(nz):
        out2[d] = second[d * nxc : (d + 1) * nxc]
    r2[0] = second[0:nxc]
    for d in range(nz - 1, 0, -1):
        push(1, out2.at[d], r2.at[d], z_off(d))

    snd, rcv = snd_ref[...], rcv_ref[...]
    t_e = iota((owners, ed), 0)
    k_t, dz_t = t_e % nxc, t_e // nxc
    p_t = (
        ((z - dz_t) & (nz - 1)) * nxc
        + ((x - (k_t >> 1)) & (nx - 1)) * 2
        + (c ^ (k_t & 1))
    )
    hot_st = hot(iota((nd, ed), 0) == snd)
    hot_ht = hot(p_t + nd == snd)
    hot_rt = hot(iota((nd, ed), 0) == rcv)

    def picked(onehot_t, table):
        high, low = two_parts(table)
        return t_dot(onehot_t, high) + t_dot(onehot_t, low)

    live = jnp.concatenate(
        [
            jnp.where(iota((block, hs_w), 0) < vc_ref[b], 1.0, 0.0)
            for b in range(ed // block)
        ],
        axis=0,
    )
    edges = e_ref[...]
    base = (
        dot(edges, win_ref[0])
        + be_ref[...]
        + picked(hot_st, dot(nodes, win_ref[1]))
        + picked(hot_rt, dot(nodes, win_ref[2]))
    )
    ge = ge_ref[...]
    wout = wout_ref[...]
    ge_w = dot_t(ge, wout)
    gn = gn_ref[...]
    gn_w = dot_t(gn, wno_ref[...])
    base_n = dot(nodes, wn_ref[0]) + bn_ref[...]

    arrived(1, r2.at[pl.ds(1, nz - 1)])
    halo = r2[...].reshape(owners, d_feat)
    pre = base + picked(hot_ht, dot(halo, win_ref[1]))
    sg = sigmoid(pre)
    hidden = (pre * sg * live).astype(BF16)
    slope = sg * (1.0 + pre * (1.0 - sg)) * live
    hs = dot(hot_rt, hidden).astype(BF16)
    hs_b[...] = hs
    for d in range(1, ny):
        push(4, hs_b, hs_g.at[d - 1], y_off(d))
    geo = t_dot(ge, hidden)
    arrived(2, wout_g)
    arrived(4, hs_g)
    agg = dot(hs, wout)
    for d in range(1, ny):
        agg += dot(hs_g[d - 1], wout_g[d - 1])
    agg = agg.astype(BF16)

    npre = base_n + dot(agg, wn_ref[1])
    nsg = sigmoid(npre)
    nhid = (npre * nsg).astype(BF16)
    npg = (gn_w * (nsg * (1.0 + npre * (1.0 - nsg)))).astype(BF16)
    npg_b[...] = npg
    for d in range(1, ny):
        push(5, npg_b, npg_g.at[d - 1], y_off(d))
    for d in range(1, ny):
        yd = pl.multiple_of(lax.rem(y + d, ny) * fs_w, fs_w)
        push(6, win_ref.at[:, pl.ds(yd, fs_w)], rows_g.at[d - 1], y_off(d))
        push(7, wn_ref.at[0, pl.ds(yd, fs_w)], wn1_g.at[d - 1], y_off(d))
    g4[...] = t_dot(gn, nhid)
    g2[0:d_feat] = t_dot(nodes, npg)
    g2[d_feat:] = t_dot(agg, npg)
    arrived(3, wn2_g)
    arrived(5, npg_g)
    grad_agg = dot_t(npg, wn_ref[1])
    for d in range(1, ny):
        grad_agg += dot_t(npg_g[d - 1], wn2_g[d - 1])
    grad_agg = grad_agg.astype(BF16)
    epg = ((ge_w + picked(hot_rt, dot_t(grad_agg, wout))) * slope).astype(BF16)
    epg_b[...] = epg
    for d in range(1, ny):
        push(8, epg_b, epg_g.at[d - 1], y_off(d))
    g3[...] = geo + t_dot(grad_agg, hs)

    ni, eo, ei = 2 * d_feat // owners, d_feat // owners, 3 * d_feat // owners
    eip = gb_f.shape[3]

    def owner(n):
        return n % 2, (n // 2) % nx, n // nxc

    for n in range(owners):
        oc, ox, oz = owner(n)
        at = ga_f.at[oc, ox, oz]
        at[0:ni] = g2[n * ni : (n + 1) * ni]
        at[ni : ni + eo] = g3[n * eo : (n + 1) * eo]
        at[ni + eo : ni + 2 * eo] = g4[n * eo : (n + 1) * eo]
    ha[...] = ga_f[...].astype(BF16)
    push(9, ha.at[1 - c], ca, by(c=1 - c))

    s_hot = dot(hot_st, epg).astype(BF16)
    h_hot = dot(hot_ht, epg).astype(BF16)
    r_hot = dot(hot_rt, epg).astype(BF16)
    g1[0:d_feat] = t_dot(edges, epg)
    g1[d_feat : 2 * d_feat] = t_dot(nodes, s_hot) + t_dot(halo, h_hot)
    g1[2 * d_feat :] = t_dot(nodes, r_hot)
    for n in range(owners):
        oc, ox, oz = owner(n)
        at = gb_f.at[oc, ox, oz]
        at[0:ei] = g1[n * ei : (n + 1) * ei]
        if eip > ei:
            at[ei:] = jnp.zeros((eip - ei, hs_w), F32)
    hb[...] = gb_f[...].astype(BF16)
    push(10, hb.at[1 - c], cb, by(c=1 - c))

    def add_core(phase, own, got, to, out, slots):
        arrived(phase, got)
        out[...] = (own[c].astype(F32) + got[...].astype(F32)).astype(BF16)
        for d in range(1, nx):
            xd = lax.rem(x + d, nx)
            push(to, out.at[xd], slots.at[d - 1], by(x=xd))

    def add_x(phase, own, got, to, out, slots):
        arrived(phase, got)
        total = own[x].astype(F32)
        for d in range(1, nx):
            total += got[d - 1].astype(F32)
        out[...] = total.astype(BF16)
        for d in range(nz - 1, 0, -1):
            zd = lax.rem(z + d, nz)
            push(to, out.at[zd], slots.at[d - 1], by(z=zd))

    def add_z(phase, own, got):
        arrived(phase, got)
        total = own[z].astype(F32)
        for d in range(1, nz):
            total += got[d - 1].astype(F32)
        return total

    add_core(9, ha, ca, 11, xa, rxa)
    add_core(10, hb, cb, 12, xb, rxb)

    mine = pl.ds(pl.multiple_of(y * fs_w, fs_w), fs_w)
    arrived(6, rows_g)
    arrived(7, wn1_g)
    arrived(8, epg_g)
    grad_e = ge_ref[:, mine].astype(F32) + dot_t(epg, win_ref[0, mine])
    to_send = dot_t(h_hot, win_ref[1, mine])
    grad_n = (
        gn_ref[:, mine].astype(F32)
        + dot_t(npg, wn_ref[0, mine])
        + dot_t(s_hot, win_ref[1, mine])
        + dot_t(r_hot, win_ref[2, mine])
    )
    for d in range(1, ny):
        part = epg_g[d - 1]
        s_d = dot(hot_st, part).astype(BF16)
        h_d = dot(hot_ht, part).astype(BF16)
        r_d = dot(hot_rt, part).astype(BF16)
        grad_e += dot_t(part, rows_g[d - 1, 0])
        to_send += dot_t(h_d, rows_g[d - 1, 1])
        grad_n += (
            dot_t(s_d, rows_g[d - 1, 1])
            + dot_t(r_d, rows_g[d - 1, 2])
            + dot_t(npg_g[d - 1], wn1_g[d - 1])
        )
    to_send = to_send.astype(BF16)
    for d in range(nz):
        s_out[d] = to_send[d * nxc : (d + 1) * nxc]
    s_a[0] = to_send[0:nxc]
    for d in range(nz - 1, 0, -1):
        push(13, s_out.at[d], s_a.at[d], z_back(d))
    o_edges[...] = grad_e.astype(BF16)

    add_x(11, xa, rxa, 14, za, rza)
    add_x(12, xb, rxb, 15, zb, rzb)

    arrived(13, s_a.at[pl.ds(1, nz - 1)])
    r_i = iota((owners, owners), 0)
    back = hot(iota((owners, owners), 1) == (r_i % nz) * nxc + r_i // nz)
    mid = dot(back, s_a[...].reshape(owners, fs_w)).astype(BF16)
    for k in range(nxc):
        s_mid[k] = mid[k * nz : (k + 1) * nz]
    s_b[0] = mid[0:nz]
    for k in range(1, nxc):
        push(16, s_mid.at[k], s_b.at[k], xc_back(k))

    total_a = add_z(14, za, rza)
    o_ni[...] = total_a[0:ni]
    turned = jnp.transpose(total_a[ni : ni + 2 * eo])
    o_eo[...] = turned[:, 0:eo]
    o_no[...] = turned[:, eo:]
    total_b = add_z(15, zb, rzb)
    o_ei[...] = total_b[0:ei]

    arrived(16, s_b.at[pl.ds(1, nxc - 1)])
    grad_n += dot(sl_perm, s_b[...].reshape(owners, fs_w))
    o_nodes[...] = grad_n.astype(BF16)

    left(0, out1.at[pl.ds(1, nxc - 1)])
    left(1, out2.at[pl.ds(1, nz - 1)])
    left(2, wout_g)
    left(3, wn2_g)
    left(4, hs_g)
    left(5, npg_g)
    left(6, rows_g)
    left(7, wn1_g)
    left(8, epg_g)
    left(9, ca)
    left(10, cb)
    left(11, rxa)
    left(12, rxb)
    left(13, s_a.at[pl.ds(1, nz - 1)])
    left(14, rza)
    left(15, rzb)
    left(16, s_b.at[pl.ds(1, nxc - 1)])


def body(nz, nx, ny, nodes, edges, gn, ge, win, be, wout, wn, bn, wno, snd, rcv, vc, sl):
    nd, d = nodes.shape
    ed = edges.shape[0]
    hw = wout.shape[0]
    fw = d // ny
    nxc = 2 * nx
    owners = nz * nxc
    ni, eo, ei = 2 * d // owners, d // owners, 3 * d // owners
    ra = ni + 2 * eo
    rb = -(-ei // 16) * 16
    vm = pltpu.VMEM
    phases = 17
    v_spec = pl.BlockSpec(memory_space=pltpu.VMEM)
    s_spec = pl.BlockSpec(memory_space=pltpu.SMEM)
    outs = pl.pallas_call(
        functools.partial(kernel, nz, nx, ny),
        out_shape=(
            jax.ShapeDtypeStruct((nd, fw), BF16),
            jax.ShapeDtypeStruct((ed, fw), BF16),
            jax.ShapeDtypeStruct((ei, hw), F32),
            jax.ShapeDtypeStruct((hw, eo), F32),
            jax.ShapeDtypeStruct((ni, hw), F32),
            jax.ShapeDtypeStruct((hw, eo), F32),
        ),
        in_specs=[v_spec] * 3 + [s_spec] + [v_spec] * 10,
        out_specs=(v_spec,) * 6,
        scratch_shapes=[
            vm((nxc, nz, d), BF16),
            vm((nxc, nz, d), BF16),
            vm((nz, nxc, d), BF16),
            vm((nz, nxc, d), BF16),
            vm((ny - 1, hw, d), BF16),
            vm((ny - 1, d, hw), BF16),
            vm((ny - 1, 3, fw, hw), BF16),
            vm((ny - 1, fw, hw), BF16),
            vm((nd, hw), BF16),
            vm((ny - 1, nd, hw), BF16),
            vm((nd, hw), BF16),
            vm((ny - 1, nd, hw), BF16),
            vm((ed, hw), BF16),
            vm((ny - 1, ed, hw), BF16),
            vm((2, nx, nz, ra, hw), F32),
            vm((2, nx, nz, rb, hw), F32),
            vm((3 * d, hw), F32),
            vm((2 * d, hw), F32),
            vm((d, hw), F32),
            vm((d, hw), F32),
            vm((2, nx, nz, ra, hw), BF16),
            vm((2, nx, nz, rb, hw), BF16),
            vm((nx, nz, ra, hw), BF16),
            vm((nx, nz, rb, hw), BF16),
            vm((nx, nz, ra, hw), BF16),
            vm((nx, nz, rb, hw), BF16),
            vm((nx - 1, nz, ra, hw), BF16),
            vm((nx - 1, nz, rb, hw), BF16),
            vm((nz, ra, hw), BF16),
            vm((nz, rb, hw), BF16),
            vm((nz - 1, ra, hw), BF16),
            vm((nz - 1, rb, hw), BF16),
            vm((nz, nxc, fw), BF16),
            vm((nz, nxc, fw), BF16),
            vm((nxc, nz, fw), BF16),
            vm((nxc, nz, fw), BF16),
            pltpu.SemaphoreType.DMA((phases,)),
            pltpu.SemaphoreType.DMA((phases,)),
        ],
        compiler_params=pltpu.CompilerParams(collective_id=0, has_side_effects=True),
    )(
        sl.reshape(1, owners),
        snd.reshape(1, ed),
        rcv.reshape(1, ed),
        vc,
        nodes,
        edges,
        gn,
        ge,
        win.reshape(3, d, hw),
        be.reshape(1, hw),
        wout,
        wn.reshape(2, d, hw),
        bn.reshape(1, hw),
        wno,
    )
    return outs


def solution(mesh):
    ny = mesh.shape["chan"]
    nx = 4 if mesh.shape["node"] == 128 else 2
    nz = mesh.shape["node"] // (2 * nx)
    split = Mesh(mesh.devices.reshape(nz, nx, 2, ny), ("z", "x", "c", "y"))
    in_specs = (
        P(NODE, None),
        P(NODE, None),
        P(NODE, None),
        P(NODE, None),
        P(None, "y"),
        P("y"),
        P("y", None),
        P(None, "y"),
        P("y"),
        P("y", None),
        P(NODE),
        P(NODE),
        P(NODE),
        P(NODE, None),
    )
    out_specs = (
        P(NODE, "y"),
        P(NODE, "y"),
        P(NODE, "y"),
        P("y", NODE),
        P(NODE, "y"),
        P("y", NODE),
    )
    return jax.shard_map(
        functools.partial(body, nz, nx, ny),
        mesh=split,
        in_specs=in_specs,
        out_specs=out_specs,
        check_vma=False,
    )
```

time: 219 us -> 73.1 us (0.33); the launches traced: 215 us -> 72.8 us
  waiting for transfers between devices: 100 us -> 0 us
  Pallas kernels: 0 us -> 65.4 us
  starting transfers between devices: 57 us -> 0 us
  blocking collectives: 17.8 us -> 0 us
  other arithmetic: 13.6 us -> 0 us
  local copies, waits for them, and re-layouts: 18.7 us -> 6.69 us
  matrix products: 6.81 us -> 0 us
    all_to_all x9 -> x0, waiting for transfers between devices: 100 us -> none  [the longest x3 35.5 us: summed_rows(): lax.all_to_all(nearer.astype(jnp.bfloat16), far, split_axis=0, concat_axi...]
    pallas_call x0 -> x1, Pallas kernels: none -> 65.4 us  [body(): pl.pallas_call(functools.partial(kernel, nz, nx, ny), out_shape=(jax.Shap...]
    all_to_all x9 -> x0, starting transfers between devices: 57 us -> none  [the longest x1 20.4 us: body(): lax.all_to_all(outgoing, NODE, split_axis=0, concat_axis=0, tiled=True)]
    all_to_all x3 -> x0, blocking collectives: 17.8 us -> none  [sum_at_owner(): lax.all_to_all(pieces, axis, split_axis=0, concat_axis=0, tiled=True)]
    gather x4 -> x0, local copies, waits for them, and re-layouts: 7.55 us -> none  [the longest x1 2.06 us: body(): nodes[receivers]]
    dot_general x11 -> x0, matrix products: 6.81 us -> none  [the longest x8 4.96 us: contract(): lax.dot_general(left_mat, right_mat, (((left_dim,), (right_dim,)), ((), (...]
    scatter-add x3 -> x0, other arithmetic: 5.75 us -> none  [seg_total(): return jax.ops.segment_sum(values, ids, num_segments=count)]
    convert_element_type x3 -> x0, other arithmetic: 3.02 us -> none  [the longest x1 1.56 us: body(): grad_edges = (own_edges + summed_edges).astype(jnp.bfloat16)]
  transfers between devices with their start and end apart: 9 -> 0, of which waited for: 9 -> 0; matrix products, arithmetic and copies ran while one was open for 11% -> 0% of each run, Pallas kernels for 0% -> 0%
where the time goes in v1:
time: 73.1 us; the launch traced here: 72.8 us
  Pallas kernels  65.4 us (89%)
  local copies, waits for them, and re-layouts  6.69 us (9%)
    pallas_call x1, Pallas kernels, body(): pl.pallas_call(functools.partial(kernel, nz, nx, ny), out_shape=(jax.Shap...  65.4 us
    unnamed x18, local copies, waits for them, and re-layouts  3.38 us
    pallas_call x2, local copies, waits for them, and re-layouts, body(): pl.pallas_call(functools.partial(kernel, nz, nx, ny), out_shape=(jax.Shap...  2.19 us

profile of v1, /device:TPU:1, one launch (start us, length us, event | category | flops | bytes accessed | tf_op | source)
XLA Modules:
  0.0 72.8 jit_solution(16635301811409126605)
XLA Ops:
  0.6 0.0 copy-start.5
  0.6 0.7 copy-done.5
  1.3 0.0 copy-start.6
  1.3 0.6 reshape.34.snd_ref
  1.9 0.1 copy-done.6
  2.0 0.6 reshape.35.rcv_ref
  2.6 65.4 %shard_map.181 = (bf16[128,128]{1,0:T(8,128)(2,1)}, bf16[384,128]{1,0:T(8,128)(2,1)}, f32[12,128]{1,0:T(8,128)}, f32[128,4]{1,0:T(8,128)}, f32[8,128]{1,0:T(8,128)}, /*index=5*/f32[128,4]{1,0:T(8,128)}) custom-call(s32[1,128]{1,0:T(1,128)} %bitcast.7, s32[1,384]{1,0:T(1,128)} %reshape.34.snd_ref, s32[1,384]{1,0:T(1,128)} %reshape.35.rcv_ref, s32[3]{0:T(128)} %vc_ref.1, ...), custom_call_target="tpu_custom_call" | custom-call | tf_op jit(solution)/shard_map/pallas_call | solution.py:415
  68.0 0.0 copy-start.1
  68.0 0.0 copy-start.2
  68.0 0.0 copy-start
  68.0 1.5 %copy.20 = f32[128,4]{0,1:T(4,128)} copy(f32[128,4]{1,0:T(8,128)} %get-tuple-element.9) | data formatting | bytes 4096 | tf_op jit(solution)/shard_map/pallas_call | solution.py:415
  69.5 0.0 copy-done.1
  69.5 0.7 copy.21
  70.2 0.0 copy-done.2
  70.2 0.6 copy.26
  70.8 0.0 copy-done
  70.8 0.0 copy-start.3
  70.8 0.6 copy.27
  71.5 0.1 copy-done.3
  71.5 0.0 copy-start.4
  71.5 0.6 copy.28
  72.1 0.1 copy-done.4
  72.2 0.6 copy.29
Async XLA Ops:
  0.6 0.7 copy-start.5
  1.3 0.7 copy-start.6
  68.0 1.6 %copy-start.1 = (f32[128,4]{1,0:T(8,128)S(1)}, f32[128,4]{1,0:T(8,128)}, u32[]{:S(2)}) copy-start(f32[128,4]{1,0:T(8,128)} %get-tuple-element.11) | copy-start | bytes 6148
  68.0 2.2 %copy-start.2 = (bf16[128,128]{1,0:T(8,128)(2,1)S(1)}, bf16[128,128]{1,0:T(8,128)(2,1)}, u32[]{:S(2)}) copy-start(bf16[128,128]{1,0:T(8,128)(2,1)} %get-tuple-element.18) | copy-start | bytes 98308
  68.0 2.8 %copy-start = (bf16[384,128]{1,0:T(8,128)(2,1)S(1)}, bf16[384,128]{1,0:T(8,128)(2,1)}, u32[]{:S(2)}) copy-start(bf16[384,128]{1,0:T(8,128)(2,1)} %get-tuple-element.19) | copy-start | bytes 294916
  70.8 0.7 copy-start.3
  71.5 0.7 copy-start.4

commit v2 on v1

--- a/solution.py
+++ b/solution.py
@@ -47,6 +47,22 @@
     nz,
     nx,
     ny,
+    sl_in,
+    snd_in,
+    rcv_in,
+    vc_in,
+    n_in,
+    e_in,
+    gn_in,
+    ge_in,
+    win_in,
+    be_in,
+    wout_in,
+    wn_in,
+    bn_in,
+    wno_in,
+    o_wide,
+    o_rows,
     sl_ref,
     snd_ref,
     rcv_ref,
@@ -61,12 +77,7 @@
     wn_ref,
     bn_ref,
     wno_ref,
-    o_nodes,
-    o_edges,
-    o_ei,
-    o_eo,
-    o_ni,
-    o_no,
+    load,
     out1,
     r1,
     out2,
@@ -133,6 +144,12 @@
     for peer in peers:
         pl.semaphore_signal(barrier, inc=1, device_id=peer, device_id_type=MESH)
 
+    sources = (sl_in, n_in, wout_in, wn_in, e_in, win_in, snd_in, rcv_in, vc_in, be_in, bn_in, ge_in, gn_in, wno_in)
+    places = (sl_ref, n_ref, wout_ref, wn_ref, e_ref, win_ref, snd_ref, rcv_ref, vc_ref, be_ref, bn_ref, ge_ref, gn_ref, wno_ref)
+    loads = [pltpu.make_async_copy(a, b, load.at[i]) for i, (a, b) in enumerate(zip(sources, places))]
+    for copy in loads:
+        copy.start()
+
     def push(phase, src, dst, peer):
         pltpu.make_async_remote_copy(
             src_ref=src,
@@ -144,11 +161,15 @@
         ).start()
 
     def arrived(phase, ref):
-        pltpu.make_async_copy(ref, ref, recv.at[phase]).wait()
+        with jax.named_scope(f"wait{phase}"):
+            pltpu.make_async_copy(ref, ref, recv.at[phase]).wait()
 
     def left(phase, ref):
         pltpu.make_async_copy(ref, ref, send.at[phase]).wait()
 
+    with jax.named_scope("load0"):
+        for copy in loads[:2]:
+            copy.wait()
     nodes = n_ref[...]
     r_q = iota((owners, owners), 1)
     k_of, dz_of = r_q // nz, r_q % nz
@@ -165,10 +186,13 @@
         out1[k] = rows_out[k * nz : (k + 1) * nz]
     r1[0] = rows_out[0:nz]
 
-    pl.semaphore_wait(barrier, len(peers))
+    with jax.named_scope("entry"):
+        pl.semaphore_wait(barrier, len(peers))
 
     for k in range(1, nxc):
         push(0, out1.at[k], r1.at[k], xc_off(k))
+    for copy in loads[2:4]:
+        copy.wait()
     for d in range(1, ny):
         push(2, wout_ref, wout_g.at[d - 1], y_off(d))
     for d in range(1, ny):
@@ -184,7 +208,9 @@
     for d in range(nz - 1, 0, -1):
         push(1, out2.at[d], r2.at[d], z_off(d))
 
-    snd, rcv = snd_ref[...], rcv_ref[...]
+    for copy in loads[4:]:
+        copy.wait()
+    snd, rcv = snd_ref[...].reshape(1, ed), rcv_ref[...].reshape(1, ed)
     t_e = iota((owners, ed), 0)
     k_t, dz_t = t_e % nxc, t_e // nxc
     p_t = (
@@ -352,7 +378,7 @@
     s_a[0] = to_send[0:nxc]
     for d in range(nz - 1, 0, -1):
         push(13, s_out.at[d], s_a.at[d], z_back(d))
-    o_edges[...] = grad_e.astype(BF16)
+    o_wide[0:ed] = grad_e.astype(BF16)
 
     add_x(11, xa, rxa, 14, za, rza)
     add_x(12, xb, rxb, 15, zb, rzb)
@@ -368,16 +394,13 @@
         push(16, s_mid.at[k], s_b.at[k], xc_back(k))
 
     total_a = add_z(14, za, rza)
-    o_ni[...] = total_a[0:ni]
-    turned = jnp.transpose(total_a[ni : ni + 2 * eo])
-    o_eo[...] = turned[:, 0:eo]
-    o_no[...] = turned[:, eo:]
+    o_rows[0 : ni + 2 * eo] = total_a
     total_b = add_z(15, zb, rzb)
-    o_ei[...] = total_b[0:ei]
+    o_rows[ni + 2 * eo :] = total_b
 
     arrived(16, s_b.at[pl.ds(1, nxc - 1)])
     grad_n += dot(sl_perm, s_b[...].reshape(owners, fs_w))
-    o_nodes[...] = grad_n.astype(BF16)
+    o_wide[ed:] = grad_n.astype(BF16)
 
     left(0, out1.at[pl.ds(1, nxc - 1)])
     left(1, out2.at[pl.ds(1, nz - 1)])
@@ -398,6 +421,16 @@
     left(16, s_b.at[pl.ds(1, nxc - 1)])
 
 
+def hand_out(wide, rows, o_nodes, o_edges, o_ei, o_eo, o_ni, o_no):
+    ed, ni, eo, ei = o_edges.shape[0], o_ni.shape[0], o_eo.shape[0], o_ei.shape[0]
+    o_edges[...] = wide[0:ed]
+    o_nodes[...] = wide[ed:]
+    o_ni[...] = rows[0:ni]
+    o_eo[...] = rows[ni : ni + eo]
+    o_no[...] = rows[ni + eo : ni + 2 * eo]
+    o_ei[...] = rows[ni + 2 * eo : ni + 2 * eo + ei]
+
+
 def body(nz, nx, ny, nodes, edges, gn, ge, win, be, wout, wn, bn, wno, snd, rcv, vc, sl):
     nd, d = nodes.shape
     ed = edges.shape[0]
@@ -411,20 +444,27 @@
     vm = pltpu.VMEM
     phases = 17
     v_spec = pl.BlockSpec(memory_space=pltpu.VMEM)
-    s_spec = pl.BlockSpec(memory_space=pltpu.SMEM)
-    outs = pl.pallas_call(
+    wide, rows = pl.pallas_call(
         functools.partial(kernel, nz, nx, ny),
-        out_shape=(
-            jax.ShapeDtypeStruct((nd, fw), BF16),
-            jax.ShapeDtypeStruct((ed, fw), BF16),
-            jax.ShapeDtypeStruct((ei, hw), F32),
-            jax.ShapeDtypeStruct((hw, eo), F32),
-            jax.ShapeDtypeStruct((ni, hw), F32),
-            jax.ShapeDtypeStruct((hw, eo), F32),
-        ),
-        in_specs=[v_spec] * 3 + [s_spec] + [v_spec] * 10,
-        out_specs=(v_spec,) * 6,
+        out_shape=(vm((ed + nd, fw), BF16), vm((ra + rb, hw), F32)),
+        in_specs=[pl.BlockSpec(memory_space=pl.ANY)] * 14,
+        out_specs=(v_spec,) * 2,
         scratch_shapes=[
+            vm((1, owners), jnp.int32),
+            vm((ed,), jnp.int32),
+            vm((ed,), jnp.int32),
+            pltpu.SMEM((vc.shape[0],), jnp.int32),
+            vm((nd, d), BF16),
+            vm((ed, d), BF16),
+            vm((nd, d), BF16),
+            vm((ed, d), BF16),
+            vm((3, d, hw), BF16),
+            vm((1, hw), F32),
+            vm((hw, d), BF16),
+            vm((2, d, hw), BF16),
+            vm((1, hw), F32),
+            vm((hw, d), BF16),
+            pltpu.SemaphoreType.DMA((14,)),
             vm((nxc, nz, d), BF16),
             vm((nxc, nz, d), BF16),
             vm((nz, nxc, d), BF16),
@@ -467,8 +507,8 @@
         compiler_params=pltpu.CompilerParams(collective_id=0, has_side_effects=True),
     )(
         sl.reshape(1, owners),
-        snd.reshape(1, ed),
-        rcv.reshape(1, ed),
+        snd,
+        rcv,
         vc,
         nodes,
         edges,
@@ -481,7 +521,20 @@
         bn.reshape(1, hw),
         wno,
     )
-    return outs
+    g_nodes, g_edges, g_ei, g_eo, g_ni, g_no = pl.pallas_call(
+        hand_out,
+        out_shape=(
+            jax.ShapeDtypeStruct((nd, fw), BF16),
+            jax.ShapeDtypeStruct((ed, fw), BF16),
+            jax.ShapeDtypeStruct((ei, hw), F32),
+            jax.ShapeDtypeStruct((eo, hw), F32),
+            jax.ShapeDtypeStruct((ni, hw), F32),
+            jax.ShapeDtypeStruct((eo, hw), F32),
+        ),
+        in_specs=[v_spec] * 2,
+        out_specs=(v_spec,) * 6,
+    )(*(pltpu.with_memory_space_constraint(v, pltpu.VMEM) for v in (wide, rows)))
+    return g_nodes, g_edges, g_ei, g_eo.T, g_ni, g_no.T
 
 
 def solution(mesh):

time: 73.1 us -> 64.8 us (0.89)
  local copies, waits for them, and re-layouts: 6.69 us -> 0 us
  Pallas kernels: 65.4 us -> 64 us
    unnamed x18 -> x0, local copies, waits for them, and re-layouts: 3.38 us -> none
    pallas_call x2 -> x0, local copies, waits for them, and re-layouts: 2.19 us -> none  [body(): pl.pallas_call(functools.partial(kernel, nz, nx, ny), out_shape=(jax.Shap...]
    pallas_call x1 -> x2, Pallas kernels: 65.4 us -> 64 us  [the longest x1 63.3 us: body(): pl.pallas_call(functools.partial(kernel, nz, nx, ny), out_shape=(vm((ed +...]
    reshape x2 -> x0, local copies, waits for them, and re-layouts: 1.13 us -> none  [the longest x1 0.56 us: body(): snd.reshape(1, ed)]
where the time goes in v2:
time: 64.8 us; the launch traced here: 64.7 us
  Pallas kernels  64 us (99%)
  between operations  0.65 us (1%)
    pallas_call x1, Pallas kernels, body(): pl.pallas_call(functools.partial(kernel, nz, nx, ny), out_shape=(vm((ed +...  63.3 us

profile of v2, /device:TPU:1, one launch (start us, length us, event | category | flops | bytes accessed | tf_op | source)
XLA Modules:
  0.0 64.7 jit_solution(10236444732536408698)
XLA Ops:
  0.6 63.3 %shard_map.181 = (bf16[512,128]{1,0:T(8,128)(2,1)S(1)}, f32[32,128]{1,0:T(8,128)S(1)}) custom-call(s32[1,128]{1,0:T(1,128)} %bitcast.9, s32[384]{0:T(512)} %snd_in.1, s32[384]{0:T(512)} %rcv_in.1, s32[3]{0:T(128)} %vc_in.1, bf16[128,512]{1,0:T(8,128)(2,1)} %n_in.1, bf16[384,512]{1,0:T(8,128)(2,1)} %e_in.1, bf16[128,512]{1,0:T(8,128)(2,1)} %gn_in.1, ...), custom_call_target="tpu_custom_call" | custom-call | tf_op jit(solution)/shard_map/pallas_call | solution.py:447
  64.0 0.7 %shard_map.182 = (bf16[128,128]{1,0:T(8,128)(2,1)}, bf16[384,128]{1,0:T(8,128)(2,1)}, f32[12,128]{1,0:T(8,128)}, f32[4,128]{1,0:T(4,128)}, f32[8,128]{1,0:T(8,128)}, /*index=5*/f32[4,128]{1,0:T(4,128)}) custom-call(bf16[512,128]{1,0:T(8,128)(2,1)S(1)} %get-tuple-element.14.wide, f32[32,128]{1,0:T(8,128)S(1)} %get-tuple-element.15.rows), custom_call_target="tpu_custom_call" | custom-call | tf_op jit(solution)/shard_map/pallas_call | solution.py:524

commit v3 on v2

v3 whole, which is shorter than its diff:
```python
import functools

import jax
import jax.numpy as jnp
from jax import lax
from jax.experimental import pallas as pl
from jax.experimental.pallas import tpu as pltpu
from jax.sharding import Mesh
from jax.sharding import PartitionSpec as P

NODE = ("z", "x", "c")
MESH = pl.DeviceIdType.MESH
F32 = jnp.float32
BF16 = jnp.bfloat16


def dot(a, b):
    return jnp.dot(a, b, preferred_element_type=F32)


def dot_t(a, b):
    return lax.dot_general(a, b, (((1,), (1,)), ((), ())), preferred_element_type=F32)


def t_dot(a, b):
    return lax.dot_general(a, b, (((0,), (0,)), ((), ())), preferred_element_type=F32)


def iota(shape, dim):
    return lax.broadcasted_iota(jnp.int32, shape, dim)


def hot(cond):
    return jnp.where(cond, 1.0, 0.0).astype(BF16)


def two_parts(v):
    high = v.astype(BF16)
    return high, (v - high.astype(F32)).astype(BF16)


def sigmoid(v):
    return 1.0 / (1.0 + jnp.exp(-v))


PHASES = (
    "halo",
    "raw1",
    "raw2",
    "wout",
    "wout_c",
    "wn2",
    "wn2_c",
    "nb",
    "rows",
    "rows_c",
    "wn1",
    "wn1_c",
    "hs",
    "epg",
    "core_a",
    "core_b",
    "x_a",
    "x_b",
    "z_a",
    "z_b",
    "back",
    "sums",
)


def kernel(
    nz,
    nx,
    ny,
    sl_in,
    snd_in,
    rcv_in,
    vc_in,
    n_in,
    e_in,
    gn_in,
    ge_in,
    win_in,
    be_in,
    wout_in,
    wn_in,
    bn_in,
    wno_in,
    o_wide,
    o_rows,
    sl_ref,
    snd_ref,
    rcv_ref,
    vc_ref,
    n_ref,
    e_ref,
    gn_ref,
    ge_ref,
    win_ref,
    be_ref,
    wout_ref,
    wn_ref,
    bn_ref,
    wno_ref,
    load,
    p_out,
    p_in,
    out1,
    r1,
    out2,
    r2,
    wout_g,
    wn2_g,
    rows_g,
    wn1_g,
    nb_b,
    nb_g,
    hs_b,
    hs_g,
    epg_b,
    epg_g,
    ga_f,
    gb_f,
    g1,
    g2,
    g3,
    g4,
    ha,
    hb,
    ca,
    cb,
    xa,
    xb,
    rxa,
    rxb,
    za,
    zb,
    rza,
    rzb,
    back_out,
    back_in,
    sums_b,
    sums_g,
    send,
    recv,
):
    z, x, c, y = (lax.axis_index(a) for a in ("z", "x", "c", "y"))
    nxc = 2 * nx
    owners = nz * nxc
    nd, d_feat = n_ref.shape
    ed = e_ref.shape[0]
    hs_w = wout_ref.shape[0]
    fs_w = d_feat // ny
    block = ed // vc_ref.shape[0]

    def by(**kw):
        return kw

    def at_xc(k, sign=1):
        place = {}
        if k // 2:
            place["x"] = lax.rem(x + nx + sign * (k // 2), nx)
        if k % 2:
            place["c"] = 1 - c
        return place

    def at_z(d, sign=1):
        return {"z": lax.rem(z + nz + sign * d, nz)} if d else {}

    def at_y(d):
        return {"y": lax.rem(y + d, ny)}

    def hops(k, d):
        return min(d, nz - d) + min(k // 2, nx - k // 2)

    everyone = [(k, d) for k in range(nxc) for d in range(nz) if k or d]
    everyone.sort(key=lambda kd: -hops(*kd))

    sources = (sl_in, n_in, win_in, wout_in, wn_in, e_in, snd_in, rcv_in, vc_in, be_in, bn_in, ge_in, gn_in, wno_in)
    places = (sl_ref, n_ref, win_ref, wout_ref, wn_ref, e_ref, snd_ref, rcv_ref, vc_ref, be_ref, bn_ref, ge_ref, gn_ref, wno_ref)
    loads = [pltpu.make_async_copy(a, b, load.at[i]) for i, (a, b) in enumerate(zip(sources, places))]

    barrier = pltpu.get_barrier_semaphore()
    peers = [at_xc(k) | at_z(d) for k, d in everyone] + [at_y(d) for d in range(1, ny)]
    for peer in peers:
        pl.semaphore_signal(barrier, inc=1, device_id=peer, device_id_type=MESH)
    for copy in loads:
        copy.start()

    def push(phase, src, dst, peer):
        pltpu.make_async_remote_copy(
            src_ref=src,
            dst_ref=dst,
            send_sem=send.at[PHASES.index(phase)],
            recv_sem=recv.at[PHASES.index(phase)],
            device_id=peer,
            device_id_type=MESH,
        ).start()

    def arrived(phase, ref):
        with jax.named_scope(f"wait_{phase}"):
            pltpu.make_async_copy(ref, ref, recv.at[PHASES.index(phase)]).wait()

    def left(phase, ref):
        pltpu.make_async_copy(ref, ref, send.at[PHASES.index(phase)]).wait()

    with jax.named_scope("load0"):
        for copy in loads[:2]:
            copy.wait()
    nodes = n_ref[...]
    r_q = iota((owners, owners), 1)
    k_of, dz_of = r_q // nz, r_q % nz
    q_of = (
        ((z + dz_of) & (nz - 1)) * nxc
        + ((x + (k_of >> 1)) & (nx - 1)) * 2
        + (c ^ (k_of & 1))
    )
    perm_q = hot(iota((owners, owners), 0) == q_of)
    sl_hot = hot(iota((nd, owners), 0) == sl_ref[...])
    sl_perm = dot(sl_hot, perm_q).astype(BF16)
    rows_out = t_dot(sl_perm, nodes).astype(BF16)
    for copy in loads[2:3]:
        copy.wait()
    p_out[...] = dot(rows_out, win_ref[1]).reshape(owners, 1, hs_w)
    p_in[0] = p_out[0]
    for k in range(nxc):
        out1[k] = rows_out[k * nz : (k + 1) * nz]
    r1[0] = rows_out[0:nz]

    with jax.named_scope("entry"):
        pl.semaphore_wait(barrier, len(peers))

    for k, d in everyone:
        push("halo", p_out.at[k * nz + d], p_in.at[k * nz + d], at_xc(k) | at_z(d))
    for k in range(1, nxc):
        push("raw1", out1.at[k], r1.at[k], at_xc(k))

    hw2, dw2, fw2 = hs_w // 2, d_feat // 2, fs_w // 2
    for copy in loads[3:5]:
        copy.wait()
    for d in range(1, ny):
        push("wout", wout_ref.at[pl.ds(c * hw2, hw2)], wout_g.at[d - 1, c], at_y(d))
    for d in range(1, ny):
        push("wn2", wn_ref.at[1, pl.ds(c * dw2, dw2)], wn2_g.at[d - 1, c], at_y(d))

    def hand_on(phase, buf):
        arrived(phase, buf.at[:, c])
        for d in range(1, ny):
            push(phase + "_c", buf.at[d - 1, c], buf.at[d - 1, c], {"c": 1 - c})

    for copy in loads[5:]:
        copy.wait()
    gn = gn_ref[...]
    gn_w = dot_t(gn, wno_ref[...])
    base_n = dot(nodes, wn_ref[0]) + bn_ref[...]
    nb_b[0] = gn_w.astype(BF16)
    nb_b[1] = base_n.astype(BF16)
    for d in range(1, ny):
        push("nb", nb_b, nb_g.at[d - 1], at_y(d))

    snd, rcv = snd_ref[...].reshape(1, ed), rcv_ref[...].reshape(1, ed)

    def remote(k, dz):
        owner_of = (
            ((z - dz) & (nz - 1)) * nxc
            + ((x - (k >> 1)) & (nx - 1)) * 2
            + (c ^ (k & 1))
        )
        return hot(owner_of + nd == snd)

    t_e = iota((owners, ed), 0)
    hot_pt = remote(t_e // nz, t_e % nz)
    hot_ht = remote(t_e % nxc, t_e // nxc)
    hot_st = hot(iota((nd, ed), 0) == snd)
    hot_rt = hot(iota((nd, ed), 0) == rcv)

    def picked(onehot_t, table):
        high, low = two_parts(table)
        return t_dot(onehot_t, high) + t_dot(onehot_t, low)

    live = jnp.concatenate(
        [
            jnp.where(iota((block, hs_w), 0) < vc_ref[b], 1.0, 0.0)
            for b in range(ed // block)
        ],
        axis=0,
    )
    edges = e_ref[...]
    base = (
        dot(edges, win_ref[0])
        + be_ref[...]
        + picked(hot_st, dot(nodes, win_ref[1]))
        + picked(hot_rt, dot(nodes, win_ref[2]))
    )
    ge = ge_ref[...]
    wout = wout_ref[...]
    ge_w = dot_t(ge, wout)

    t_i = iota((owners, owners), 0)
    stage = hot(iota((owners, owners), 1) == (t_i % nxc) * nz + t_i // nxc)
    arrived("raw1", r1.at[pl.ds(1, nxc - 1)])
    second = dot(stage, r1[...].reshape(owners, d_feat)).astype(BF16)
    for d in range(nz):
        out2[d] = second[d * nxc : (d + 1) * nxc]
    r2[0] = second[0:nxc]
    for d in range(nz - 1, 0, -1):
        push("raw2", out2.at[d], r2.at[d], at_z(d))
    hand_on("wout", wout_g)

    arrived("halo", p_in.at[pl.ds(1, owners - 1)])
    pre = base + picked(hot_pt, p_in[...].reshape(owners, hs_w))
    sg = sigmoid(pre)
    hidden = (pre * sg * live).astype(BF16)
    slope = sg * (1.0 + pre * (1.0 - sg)) * live
    hs = dot(hot_rt, hidden).astype(BF16)
    hs_b[...] = hs
    for d in range(1, ny):
        push("hs", hs_b, hs_g.at[d - 1], at_y(d))
    hand_on("wn2", wn2_g)
    geo = t_dot(ge, hidden)
    wn2 = wn_ref[1]
    arrived("wout_c", wout_g.at[:, 1 - c])
    arrived("hs", hs_g)
    for d in range(1, ny):
        yd = pl.multiple_of(lax.rem(y + d, ny) * fs_w + c * fw2, fw2)
        push("rows", win_ref.at[:, pl.ds(yd, fw2)], rows_g.at[d - 1, c], at_y(d))
        push("wn1", wn_ref.at[0, pl.ds(yd, fw2)], wn1_g.at[d - 1, c], at_y(d))
    agg = dot(hs, wout)
    for d in range(1, ny):
        agg += dot(hs_g[d - 1], wout_g[d - 1].reshape(hs_w, d_feat))
    agg = agg.astype(BF16)

    arrived("wn2_c", wn2_g.at[:, 1 - c])
    arrived("nb", nb_g)

    def unit_grad(before, gradient, weight):
        npre = before + dot(agg, weight)
        nsg = sigmoid(npre)
        slope = nsg * (1.0 + npre * (1.0 - nsg))
        return npre * nsg, (gradient * slope).astype(BF16)

    nhid, npg = unit_grad(base_n, gn_w, wn2)
    nhid = nhid.astype(BF16)
    npgs = [npg]
    grad_agg = dot_t(npg, wn2)
    for d in range(1, ny):
        weight = wn2_g[d - 1].reshape(d_feat, hs_w)
        _, other = unit_grad(
            nb_g[d - 1, 1].astype(F32), nb_g[d - 1, 0].astype(F32), weight
        )
        npgs.append(other)
        grad_agg += dot_t(other, weight)
    grad_agg = grad_agg.astype(BF16)

    ni, eo, ei = 2 * d_feat // owners, d_feat // owners, 3 * d_feat // owners

    def owner(n):
        return n % 2, (n // 2) % nx, n // nxc

    def for_owners(blocks, sources, out):
        rows = sum(size for size, _ in sources)
        for n in range(owners):
            oc, ox, oz = owner(n)
            at, start = blocks.at[oc, ox, oz], 0
            for size, source in sources:
                at[start : start + size] = source[n * size : (n + 1) * size]
                start += size
            if rows < blocks.shape[3]:
                at[rows:] = jnp.zeros((blocks.shape[3] - rows, hs_w), F32)
        out[...] = blocks[...].astype(BF16)

    g4[...] = t_dot(gn, nhid)
    g2[0:d_feat] = t_dot(nodes, npg)
    g2[d_feat:] = t_dot(agg, npg)
    for_owners(ga_f, ((ni, g2), (eo, g4)), ha)
    push("core_a", ha.at[1 - c], ca, {"c": 1 - c})

    epg = ((ge_w + picked(hot_rt, dot_t(grad_agg, wout))) * slope).astype(BF16)
    epg_b[...] = epg
    for d in range(1, ny):
        push("epg", epg_b, epg_g.at[d - 1], at_y(d))

    def add_core(phase, own, got, to, out, slots):
        arrived(phase, got)
        out[...] = (own[c].astype(F32) + got[...].astype(F32)).astype(BF16)
        for d in range(1, nx):
            xd = lax.rem(x + d, nx)
            push(to, out.at[xd], slots.at[d - 1], {"x": xd})

    def add_x(phase, own, got, to, out, slots):
        arrived(phase, got)
        total = own[x].astype(F32)
        for d in range(1, nx):
            total += got[d - 1].astype(F32)
        out[...] = total.astype(BF16)
        for d in range(nz - 1, 0, -1):
            zd = lax.rem(z + d, nz)
            push(to, out.at[zd], slots.at[d - 1], {"z": zd})

    def add_z(phase, own, got):
        arrived(phase, got)
        total = own[z].astype(F32)
        for d in range(1, nz):
            total += got[d - 1].astype(F32)
        return total

    add_core("core_a", ha, ca, "x_a", xa, rxa)

    s_sum = dot(hot_st, epg)
    s_hot = s_sum.astype(BF16)
    h_hot = dot(hot_ht, epg).astype(BF16)
    r_hot = dot(hot_rt, epg).astype(BF16)
    g3[...] = geo + t_dot(grad_agg, hs)
    g1[0:d_feat] = t_dot(edges, epg)
    g1[2 * d_feat :] = t_dot(nodes, r_hot)
    arrived("raw2", r2.at[pl.ds(1, nz - 1)])
    halo = r2[...].reshape(owners, d_feat)
    g1[d_feat : 2 * d_feat] = t_dot(nodes, s_hot) + t_dot(halo, h_hot)
    for_owners(gb_f, ((ei, g1), (eo, g3)), hb)
    push("core_b", hb.at[1 - c], cb, {"c": 1 - c})

    back_out[...] = dot(hot_pt, epg).reshape(owners, 1, hs_w)
    back_in[0] = back_out[0]
    for k, d in everyone:
        at = k * nz + d
        push("back", back_out.at[at], back_in.at[at], at_xc(k, -1) | at_z(d, -1))
    add_core("core_b", hb, cb, "x_b", xb, rxb)
    hand_on("rows", rows_g)
    hand_on("wn1", wn1_g)

    mine = pl.ds(pl.multiple_of(y * fs_w, fs_w), fs_w)
    arrived("epg", epg_g)
    arrived("rows_c", rows_g.at[:, 1 - c])
    arrived("wn1_c", wn1_g.at[:, 1 - c])
    w_s = [win_ref[1, mine]]
    grad_e = ge_ref[:, mine].astype(F32) + dot_t(epg, win_ref[0, mine])
    grad_n = (
        gn_ref[:, mine].astype(F32)
        + dot_t(npg, wn_ref[0, mine])
        + dot_t(r_hot, win_ref[2, mine])
    )
    for d in range(1, ny):
        part = epg_g[d - 1]
        r_d = dot(hot_rt, part).astype(BF16)
        w_e, w_sender, w_r = (
            jnp.concatenate([rows_g[d - 1, 0, b], rows_g[d - 1, 1, b]], axis=0)
            for b in range(3)
        )
        w_s.append(w_sender)
        grad_e += dot_t(part, w_e)
        grad_n += dot_t(r_d, w_r) + dot_t(npgs[d], wn1_g[d - 1].reshape(fs_w, hs_w))
    o_wide[0:ed] = grad_e.astype(BF16)

    add_x("x_a", xa, rxa, "z_a", za, rza)
    add_x("x_b", xb, rxb, "z_b", zb, rzb)

    arrived("back", back_in.at[pl.ds(1, owners - 1)])
    high, low = two_parts(back_in[...].reshape(owners, hs_w))
    sums = (s_sum + dot(sl_perm, high) + dot(sl_perm, low)).astype(BF16)
    sums_b[...] = sums
    for d in range(1, ny):
        push("sums", sums_b, sums_g.at[d - 1], at_y(d))
    total_a = add_z("z_a", za, rza)
    o_rows[0 : total_a.shape[0]] = total_a
    grad_n += dot_t(sums, w_s[0])
    arrived("sums", sums_g)
    for d in range(1, ny):
        grad_n += dot_t(sums_g[d - 1], w_s[d])
    o_wide[ed:] = grad_n.astype(BF16)
    total_b = add_z("z_b", zb, rzb)
    o_rows[total_a.shape[0] :] = total_b

    left("halo", p_in.at[pl.ds(1, owners - 1)])
    left("raw1", out1.at[pl.ds(1, nxc - 1)])
    left("raw2", out2.at[pl.ds(1, nz - 1)])
    for phase, buf in (
        ("wout", wout_g),
        ("wn2", wn2_g),
        ("rows", rows_g),
        ("wn1", wn1_g),
    ):
        left(phase, buf.at[:, c])
        left(phase + "_c", buf.at[:, c])
    left("nb", nb_g)
    left("hs", hs_g)
    left("epg", epg_g)
    left("core_a", ca)
    left("core_b", cb)
    left("x_a", rxa)
    left("x_b", rxb)
    left("z_a", rza)
    left("z_b", rzb)
    left("back", back_in.at[pl.ds(1, owners - 1)])
    left("sums", sums_g)


def hand_out(wide, rows, o_nodes, o_edges, o_ei, o_eo, o_ni, o_no):
    ed, ni, eo, ei = o_edges.shape[0], o_ni.shape[0], o_eo.shape[0], o_ei.shape[0]
    second = rows.shape[0] - ei - eo
    o_edges[...] = wide[0:ed]
    o_nodes[...] = wide[ed:]
    o_ni[...] = rows[0:ni]
    o_no[...] = rows[ni : ni + eo]
    o_ei[...] = rows[second : second + ei]
    o_eo[...] = rows[second + ei :]


def body(nz, nx, ny, nodes, edges, gn, ge, win, be, wout, wn, bn, wno, snd, rcv, vc, sl):
    nd, d = nodes.shape
    ed = edges.shape[0]
    hw = wout.shape[0]
    fw = d // ny
    nxc = 2 * nx
    owners = nz * nxc
    ni, eo, ei = 2 * d // owners, d // owners, 3 * d // owners
    ra = -(-(ni + eo) // 16) * 16
    rb = ei + eo
    vm = pltpu.VMEM
    phases = len(PHASES)
    v_spec = pl.BlockSpec(memory_space=pltpu.VMEM)
    wide, rows = pl.pallas_call(
        functools.partial(kernel, nz, nx, ny),
        out_shape=(vm((ed + nd, fw), BF16), vm((ra + rb, hw), F32)),
        in_specs=[pl.BlockSpec(memory_space=pl.ANY)] * 14,
        out_specs=(v_spec,) * 2,
        scratch_shapes=[
            vm((1, owners), jnp.int32),
            vm((ed,), jnp.int32),
            vm((ed,), jnp.int32),
            pltpu.SMEM((vc.shape[0],), jnp.int32),
            vm((nd, d), BF16),
            vm((ed, d), BF16),
            vm((nd, d), BF16),
            vm((ed, d), BF16),
            vm((3, d, hw), BF16),
            vm((1, hw), F32),
            vm((hw, d), BF16),
            vm((2, d, hw), BF16),
            vm((1, hw), F32),
            vm((hw, d), BF16),
            pltpu.SemaphoreType.DMA((14,)),
            vm((owners, 1, hw), F32),
            vm((owners, 1, hw), F32),
            vm((nxc, nz, d), BF16),
            vm((nxc, nz, d), BF16),
            vm((nz, nxc, d), BF16),
            vm((nz, nxc, d), BF16),
            vm((ny - 1, 2, hw // 2, d), BF16),
            vm((ny - 1, 2, d // 2, hw), BF16),
            vm((ny - 1, 2, 3, fw // 2, hw), BF16),
            vm((ny - 1, 2, fw // 2, hw), BF16),
            vm((2, nd, hw), BF16),
            vm((ny - 1, 2, nd, hw), BF16),
            vm((nd, hw), BF16),
            vm((ny - 1, nd, hw), BF16),
            vm((ed, hw), BF16),
            vm((ny - 1, ed, hw), BF16),
            vm((2, nx, nz, ra, hw), F32),
            vm((2, nx, nz, rb, hw), F32),
            vm((3 * d, hw), F32),
            vm((2 * d, hw), F32),
            vm((d, hw), F32),
            vm((d, hw), F32),
            vm((2, nx, nz, ra, hw), BF16),
            vm((2, nx, nz, rb, hw), BF16),
            vm((nx, nz, ra, hw), BF16),
            vm((nx, nz, rb, hw), BF16),
            vm((nx, nz, ra, hw), BF16),
            vm((nx, nz, rb, hw), BF16),
            vm((nx - 1, nz, ra, hw), BF16),
            vm((nx - 1, nz, rb, hw), BF16),
            vm((nz, ra, hw), BF16),
            vm((nz, rb, hw), BF16),
            vm((nz - 1, ra, hw), BF16),
            vm((nz - 1, rb, hw), BF16),
            vm((owners, 1, hw), F32),
            vm((owners, 1, hw), F32),
            vm((nd, hw), BF16),
            vm((ny - 1, nd, hw), BF16),
            pltpu.SemaphoreType.DMA((phases,)),
            pltpu.SemaphoreType.DMA((phases,)),
        ],
        compiler_params=pltpu.CompilerParams(collective_id=0, has_side_effects=True),
    )(
        sl.reshape(1, owners),
        snd,
        rcv,
        vc,
        nodes,
        edges,
        gn,
        ge,
        win.reshape(3, d, hw),
        be.reshape(1, hw),
        wout,
        wn.reshape(2, d, hw),
        bn.reshape(1, hw),
        wno,
    )
    g_nodes, g_edges, g_ei, g_eo, g_ni, g_no = pl.pallas_call(
        hand_out,
        out_shape=(
            jax.ShapeDtypeStruct((nd, fw), BF16),
            jax.ShapeDtypeStruct((ed, fw), BF16),
            jax.ShapeDtypeStruct((ei, hw), F32),
            jax.ShapeDtypeStruct((eo, hw), F32),
            jax.ShapeDtypeStruct((ni, hw), F32),
            jax.ShapeDtypeStruct((eo, hw), F32),
        ),
        in_specs=[v_spec] * 2,
        out_specs=(v_spec,) * 6,
    )(*(pltpu.with_memory_space_constraint(v, pltpu.VMEM) for v in (wide, rows)))
    return g_nodes, g_edges, g_ei, g_eo.T, g_ni, g_no.T


def solution(mesh):
    ny = mesh.shape["chan"]
    nx = 4 if mesh.shape["node"] == 128 else 2
    nz = mesh.shape["node"] // (2 * nx)
    split = Mesh(mesh.devices.reshape(nz, nx, 2, ny), ("z", "x", "c", "y"))
    in_specs = (
        P(NODE, None),
        P(NODE, None),
        P(NODE, None),
        P(NODE, None),
        P(None, "y"),
        P("y"),
        P("y", None),
        P(None, "y"),
        P("y"),
        P("y", None),
        P(NODE),
        P(NODE),
        P(NODE),
        P(NODE, None),
    )
    out_specs = (
        P(NODE, "y"),
        P(NODE, "y"),
        P(NODE, "y"),
        P("y", NODE),
        P(NODE, "y"),
        P("y", NODE),
    )
    return jax.shard_map(
        functools.partial(body, nz, nx, ny),
        mesh=split,
        in_specs=in_specs,
        out_specs=out_specs,
        check_vma=False,
    )
```

time: 64.8 us -> 52.8 us (0.81)
  Pallas kernels: 64 us -> 52.1 us
    pallas_call x1, Pallas kernels: 63.3 us -> 51.4 us  [body(): pl.pallas_call(functools.partial(kernel, nz, nx, ny), out_shape=(vm((ed +...]
where the time goes in v3:
time: 52.8 us; the launch traced here: 52.7 us
  Pallas kernels  52.1 us (99%)
  between operations  0.65 us (1%)
    pallas_call x1, Pallas kernels, body(): pl.pallas_call(functools.partial(kernel, nz, nx, ny), out_shape=(vm((ed +...  51.4 us

profile of v3, /device:TPU:1, one launch (start us, length us, event | category | flops | bytes accessed | tf_op | source)
XLA Modules:
  0.0 52.7 jit_solution(6304034468720471246)
XLA Ops:
  0.6 51.4 %shard_map.181 = (bf16[512,128]{1,0:T(8,128)(2,1)S(1)}, f32[32,128]{1,0:T(8,128)S(1)}) custom-call(s32[1,128]{1,0:T(1,128)} %bitcast.9, s32[384]{0:T(512)} %snd_in.1, s32[384]{0:T(512)} %rcv_in.1, s32[3]{0:T(128)} %vc_in.1, bf16[128,512]{1,0:T(8,128)(2,1)} %n_in.1, bf16[384,512]{1,0:T(8,128)(2,1)} %e_in.1, bf16[128,512]{1,0:T(8,128)(2,1)} %gn_in.1, ...), custom_call_target="tpu_custom_call" | custom-call | tf_op jit(solution)/shard_map/pallas_call | solution.py:522
  52.0 0.7 %shard_map.182 = (bf16[128,128]{1,0:T(8,128)(2,1)}, bf16[384,128]{1,0:T(8,128)(2,1)}, f32[12,128]{1,0:T(8,128)}, f32[4,128]{1,0:T(4,128)}, f32[8,128]{1,0:T(8,128)}, /*index=5*/f32[4,128]{1,0:T(4,128)}) custom-call(bf16[512,128]{1,0:T(8,128)(2,1)S(1)} %get-tuple-element.14.wide, f32[32,128]{1,0:T(8,128)S(1)} %get-tuple-element.15.rows), custom_call_target="tpu_custom_call" | custom-call | tf_op jit(solution)/shard_map/pallas_call | solution.py:601

commit v4 on v3

--- a/solution.py
+++ b/solution.py
@@ -142,6 +142,11 @@
     back_in,
     sums_b,
     sums_g,
+    hot_p,
+    hot_r,
+    n_t,
+    gn_t,
+    e_t,
     send,
     recv,
 ):
@@ -174,6 +179,9 @@
     def hops(k, d):
         return min(d, nz - d) + min(k // 2, nx - k // 2)
 
+    def far_first(n):
+        return sorted(range(1, n), key=lambda d: -min(d, n - d))
+
     everyone = [(k, d) for k in range(nxc) for d in range(nz) if k or d]
     everyone.sort(key=lambda kd: -hops(*kd))
 
@@ -239,14 +247,14 @@
     hw2, dw2, fw2 = hs_w // 2, d_feat // 2, fs_w // 2
     for copy in loads[3:5]:
         copy.wait()
-    for d in range(1, ny):
+    for d in far_first(ny):
         push("wout", wout_ref.at[pl.ds(c * hw2, hw2)], wout_g.at[d - 1, c], at_y(d))
-    for d in range(1, ny):
+    for d in far_first(ny):
         push("wn2", wn_ref.at[1, pl.ds(c * dw2, dw2)], wn2_g.at[d - 1, c], at_y(d))
 
     def hand_on(phase, buf):
         arrived(phase, buf.at[:, c])
-        for d in range(1, ny):
+        for d in far_first(ny):
             push(phase + "_c", buf.at[d - 1, c], buf.at[d - 1, c], {"c": 1 - c})
 
     for copy in loads[5:]:
@@ -256,7 +264,7 @@
     base_n = dot(nodes, wn_ref[0]) + bn_ref[...]
     nb_b[0] = gn_w.astype(BF16)
     nb_b[1] = base_n.astype(BF16)
-    for d in range(1, ny):
+    for d in far_first(ny):
         push("nb", nb_b, nb_g.at[d - 1], at_y(d))
 
     snd, rcv = snd_ref[...].reshape(1, ed), rcv_ref[...].reshape(1, ed)
@@ -275,9 +283,12 @@
     hot_st = hot(iota((nd, ed), 0) == snd)
     hot_rt = hot(iota((nd, ed), 0) == rcv)
 
-    def picked(onehot_t, table):
+    def picked(onehot, table):
         high, low = two_parts(table)
-        return t_dot(onehot_t, high) + t_dot(onehot_t, low)
+        return dot(onehot, high) + dot(onehot, low)
+
+    hot_p[...] = jnp.transpose(hot_pt)
+    hot_r[...] = jnp.transpose(hot_rt)
 
     live = jnp.concatenate(
         [
@@ -290,12 +301,16 @@
     base = (
         dot(edges, win_ref[0])
         + be_ref[...]
-        + picked(hot_st, dot(nodes, win_ref[1]))
-        + picked(hot_rt, dot(nodes, win_ref[2]))
+        + picked(jnp.transpose(hot_st), dot(nodes, win_ref[1]))
+        + picked(hot_r[...], dot(nodes, win_ref[2]))
     )
     ge = ge_ref[...]
     wout = wout_ref[...]
     ge_w = dot_t(ge, wout)
+
+    n_t[...] = jnp.transpose(nodes)
+    gn_t[...] = jnp.transpose(gn)
+    e_t[...] = jnp.transpose(edges)
 
     t_i = iota((owners, owners), 0)
     stage = hot(iota((owners, owners), 1) == (t_i % nxc) * nz + t_i // nxc)
@@ -304,25 +319,25 @@
     for d in range(nz):
         out2[d] = second[d * nxc : (d + 1) * nxc]
     r2[0] = second[0:nxc]
-    for d in range(nz - 1, 0, -1):
+    for d in far_first(nz):
         push("raw2", out2.at[d], r2.at[d], at_z(d))
     hand_on("wout", wout_g)
 
     arrived("halo", p_in.at[pl.ds(1, owners - 1)])
-    pre = base + picked(hot_pt, p_in[...].reshape(owners, hs_w))
+    pre = base + picked(hot_p[...], p_in[...].reshape(owners, hs_w))
     sg = sigmoid(pre)
     hidden = (pre * sg * live).astype(BF16)
     slope = sg * (1.0 + pre * (1.0 - sg)) * live
     hs = dot(hot_rt, hidden).astype(BF16)
     hs_b[...] = hs
-    for d in range(1, ny):
+    for d in far_first(ny):
         push("hs", hs_b, hs_g.at[d - 1], at_y(d))
     hand_on("wn2", wn2_g)
     geo = t_dot(ge, hidden)
     wn2 = wn_ref[1]
     arrived("wout_c", wout_g.at[:, 1 - c])
     arrived("hs", hs_g)
-    for d in range(1, ny):
+    for d in far_first(ny):
         yd = pl.multiple_of(lax.rem(y + d, ny) * fs_w + c * fw2, fw2)
         push("rows", win_ref.at[:, pl.ds(yd, fw2)], rows_g.at[d - 1, c], at_y(d))
         push("wn1", wn_ref.at[0, pl.ds(yd, fw2)], wn1_g.at[d - 1, c], at_y(d))
@@ -359,32 +374,34 @@
         return n % 2, (n // 2) % nx, n // nxc
 
     def for_owners(blocks, sources, out):
-        rows = sum(size for size, _ in sources)
         for n in range(owners):
             oc, ox, oz = owner(n)
             at, start = blocks.at[oc, ox, oz], 0
             for size, source in sources:
-                at[start : start + size] = source[n * size : (n + 1) * size]
+                if len(blocks.shape) == 5:
+                    at[start : start + size] = source[n * size : (n + 1) * size]
+                else:
+                    for row in range(0, size, 4):
+                        four = source[n * size + row : n * size + row + 4]
+                        at[(start + row) // 4] = four
                 start += size
-            if rows < blocks.shape[3]:
-                at[rows:] = jnp.zeros((blocks.shape[3] - rows, hs_w), F32)
         out[...] = blocks[...].astype(BF16)
 
-    g4[...] = t_dot(gn, nhid)
-    g2[0:d_feat] = t_dot(nodes, npg)
+    g4[...] = dot(gn_t[...], nhid)
+    g2[0:d_feat] = dot(n_t[...], npg)
     g2[d_feat:] = t_dot(agg, npg)
     for_owners(ga_f, ((ni, g2), (eo, g4)), ha)
     push("core_a", ha.at[1 - c], ca, {"c": 1 - c})
 
-    epg = ((ge_w + picked(hot_rt, dot_t(grad_agg, wout))) * slope).astype(BF16)
+    epg = ((ge_w + picked(hot_r[...], dot_t(grad_agg, wout))) * slope).astype(BF16)
     epg_b[...] = epg
-    for d in range(1, ny):
+    for d in far_first(ny):
         push("epg", epg_b, epg_g.at[d - 1], at_y(d))
 
     def add_core(phase, own, got, to, out, slots):
         arrived(phase, got)
         out[...] = (own[c].astype(F32) + got[...].astype(F32)).astype(BF16)
-        for d in range(1, nx):
+        for d in far_first(nx):
             xd = lax.rem(x + d, nx)
             push(to, out.at[xd], slots.at[d - 1], {"x": xd})
 
@@ -394,7 +411,7 @@
         for d in range(1, nx):
             total += got[d - 1].astype(F32)
         out[...] = total.astype(BF16)
-        for d in range(nz - 1, 0, -1):
+        for d in far_first(nz):
             zd = lax.rem(z + d, nz)
             push(to, out.at[zd], slots.at[d - 1], {"z": zd})
 
@@ -405,29 +422,29 @@
             total += got[d - 1].astype(F32)
         return total
 
-    add_core("core_a", ha, ca, "x_a", xa, rxa)
-
     s_sum = dot(hot_st, epg)
     s_hot = s_sum.astype(BF16)
     h_hot = dot(hot_ht, epg).astype(BF16)
     r_hot = dot(hot_rt, epg).astype(BF16)
     g3[...] = geo + t_dot(grad_agg, hs)
-    g1[0:d_feat] = t_dot(edges, epg)
-    g1[2 * d_feat :] = t_dot(nodes, r_hot)
+    g1[0:d_feat] = dot(e_t[...], epg)
+    g1[2 * d_feat :] = dot(n_t[...], r_hot)
     arrived("raw2", r2.at[pl.ds(1, nz - 1)])
     halo = r2[...].reshape(owners, d_feat)
-    g1[d_feat : 2 * d_feat] = t_dot(nodes, s_hot) + t_dot(halo, h_hot)
+    g1[d_feat : 2 * d_feat] = dot(n_t[...], s_hot) + t_dot(halo, h_hot)
     for_owners(gb_f, ((ei, g1), (eo, g3)), hb)
     push("core_b", hb.at[1 - c], cb, {"c": 1 - c})
+    add_core("core_a", ha, ca, "x_a", xa, rxa)
 
     back_out[...] = dot(hot_pt, epg).reshape(owners, 1, hs_w)
     back_in[0] = back_out[0]
+    add_core("core_b", hb, cb, "x_b", xb, rxb)
     for k, d in everyone:
         at = k * nz + d
         push("back", back_out.at[at], back_in.at[at], at_xc(k, -1) | at_z(d, -1))
-    add_core("core_b", hb, cb, "x_b", xb, rxb)
     hand_on("rows", rows_g)
     hand_on("wn1", wn1_g)
+    add_x("x_a", xa, rxa, "z_a", za, rza)
 
     mine = pl.ds(pl.multiple_of(y * fs_w, fs_w), fs_w)
     arrived("epg", epg_g)
@@ -452,25 +469,22 @@
         grad_n += dot_t(r_d, w_r) + dot_t(npgs[d], wn1_g[d - 1].reshape(fs_w, hs_w))
     o_wide[0:ed] = grad_e.astype(BF16)
 
-    add_x("x_a", xa, rxa, "z_a", za, rza)
     add_x("x_b", xb, rxb, "z_b", zb, rzb)
 
     arrived("back", back_in.at[pl.ds(1, owners - 1)])
     high, low = two_parts(back_in[...].reshape(owners, hs_w))
     sums = (s_sum + dot(sl_perm, high) + dot(sl_perm, low)).astype(BF16)
     sums_b[...] = sums
-    for d in range(1, ny):
+    for d in far_first(ny):
         push("sums", sums_b, sums_g.at[d - 1], at_y(d))
     total_a = add_z("z_a", za, rza)
-    o_rows[0 : total_a.shape[0]] = total_a
+    for i in range(total_a.shape[0]):
+        o_rows[4 * i : 4 * i + 4] = total_a[i]
     grad_n += dot_t(sums, w_s[0])
     arrived("sums", sums_g)
     for d in range(1, ny):
         grad_n += dot_t(sums_g[d - 1], w_s[d])
     o_wide[ed:] = grad_n.astype(BF16)
-    total_b = add_z("z_b", zb, rzb)
-    o_rows[total_a.shape[0] :] = total_b
-
     left("halo", p_in.at[pl.ds(1, owners - 1)])
     left("raw1", out1.at[pl.ds(1, nxc - 1)])
     left("raw2", out2.at[pl.ds(1, nz - 1)])
@@ -494,6 +508,9 @@
     left("back", back_in.at[pl.ds(1, owners - 1)])
     left("sums", sums_g)
 
+    total_b = add_z("z_b", zb, rzb)
+    o_rows[ni + eo :] = total_b
+
 
 def hand_out(wide, rows, o_nodes, o_edges, o_ei, o_eo, o_ni, o_no):
     ed, ni, eo, ei = o_edges.shape[0], o_ni.shape[0], o_eo.shape[0], o_ei.shape[0]
@@ -514,14 +531,14 @@
     nxc = 2 * nx
     owners = nz * nxc
     ni, eo, ei = 2 * d // owners, d // owners, 3 * d // owners
-    ra = -(-(ni + eo) // 16) * 16
+    ra = (ni + eo) // 4
     rb = ei + eo
     vm = pltpu.VMEM
     phases = len(PHASES)
     v_spec = pl.BlockSpec(memory_space=pltpu.VMEM)
     wide, rows = pl.pallas_call(
         functools.partial(kernel, nz, nx, ny),
-        out_shape=(vm((ed + nd, fw), BF16), vm((ra + rb, hw), F32)),
+        out_shape=(vm((ed + nd, fw), BF16), vm((4 * ra + rb, hw), F32)),
         in_specs=[pl.BlockSpec(memory_space=pl.ANY)] * 14,
         out_specs=(v_spec,) * 2,
         scratch_shapes=[
@@ -556,28 +573,33 @@
             vm((ny - 1, nd, hw), BF16),
             vm((ed, hw), BF16),
             vm((ny - 1, ed, hw), BF16),
-            vm((2, nx, nz, ra, hw), F32),
+            vm((2, nx, nz, ra, 4, hw), F32),
             vm((2, nx, nz, rb, hw), F32),
             vm((3 * d, hw), F32),
             vm((2 * d, hw), F32),
             vm((d, hw), F32),
             vm((d, hw), F32),
-            vm((2, nx, nz, ra, hw), BF16),
+            vm((2, nx, nz, ra, 4, hw), BF16),
             vm((2, nx, nz, rb, hw), BF16),
-            vm((nx, nz, ra, hw), BF16),
+            vm((nx, nz, ra, 4, hw), BF16),
             vm((nx, nz, rb, hw), BF16),
-            vm((nx, nz, ra, hw), BF16),
+            vm((nx, nz, ra, 4, hw), BF16),
             vm((nx, nz, rb, hw), BF16),
-            vm((nx - 1, nz, ra, hw), BF16),
+            vm((nx - 1, nz, ra, 4, hw), BF16),
             vm((nx - 1, nz, rb, hw), BF16),
-            vm((nz, ra, hw), BF16),
+            vm((nz, ra, 4, hw), BF16),
             vm((nz, rb, hw), BF16),
-            vm((nz - 1, ra, hw), BF16),
+            vm((nz - 1, ra, 4, hw), BF16),
             vm((nz - 1, rb, hw), BF16),
             vm((owners, 1, hw), F32),
             vm((owners, 1, hw), F32),
             vm((nd, hw), BF16),
             vm((ny - 1, nd, hw), BF16),
+            vm((ed, owners), BF16),
+            vm((ed, nd), BF16),
+            vm((d, nd), BF16),
+            vm((d, nd), BF16),
+            vm((d, ed), BF16),
             pltpu.SemaphoreType.DMA((phases,)),
             pltpu.SemaphoreType.DMA((phases,)),
         ],

time: 52.8 us -> 51.3 us (0.972)
  Pallas kernels: 52.1 us -> 50.6 us
    pallas_call x1, Pallas kernels: 51.4 us -> 49.9 us  [body(): pl.pallas_call(functools.partial(kernel, nz, nx, ny), out_shape=(vm((ed +...]
where the time goes in v4:
time: 51.3 us; the launch traced here: 51.2 us
  Pallas kernels  50.6 us (99%)
  between operations  0.65 us (1%)
    pallas_call x1, Pallas kernels, body(): pl.pallas_call(functools.partial(kernel, nz, nx, ny), out_shape=(vm((ed +...  49.9 us

profile of v4, /device:TPU:1, one launch (start us, length us, event | category | flops | bytes accessed | tf_op | source)
XLA Modules:
  0.0 51.2 jit_solution(10619084230759963345)
XLA Ops:
  0.6 49.9 %shard_map.181 = (bf16[512,128]{1,0:T(8,128)(2,1)S(1)}, f32[28,128]{1,0:T(8,128)S(1)}) custom-call(s32[1,128]{1,0:T(1,128)} %bitcast.9, s32[384]{0:T(512)} %snd_in.1, s32[384]{0:T(512)} %rcv_in.1, s32[3]{0:T(128)} %vc_in.1, bf16[128,512]{1,0:T(8,128)(2,1)} %n_in.1, bf16[384,512]{1,0:T(8,128)(2,1)} %e_in.1, bf16[128,512]{1,0:T(8,128)(2,1)} %gn_in.1, ...), custom_call_target="tpu_custom_call" | custom-call | tf_op jit(solution)/shard_map/pallas_call | solution.py:539
  50.5 0.7 %shard_map.182 = (bf16[128,128]{1,0:T(8,128)(2,1)}, bf16[384,128]{1,0:T(8,128)(2,1)}, f32[12,128]{1,0:T(8,128)}, f32[4,128]{1,0:T(4,128)}, f32[8,128]{1,0:T(8,128)}, /*index=5*/f32[4,128]{1,0:T(4,128)}) custom-call(bf16[512,128]{1,0:T(8,128)(2,1)S(1)} %get-tuple-element.14.wide, f32[28,128]{1,0:T(8,128)S(1)} %get-tuple-element.15.rows), custom_call_target="tpu_custom_call" | custom-call | tf_op jit(solution)/shard_map/pallas_call | solution.py:623

commit v5 on v4

--- a/solution.py
+++ b/solution.py
@@ -120,12 +120,9 @@
     hs_g,
     epg_b,
     epg_g,
-    ga_f,
     gb_f,
     g1,
-    g2,
     g3,
-    g4,
     ha,
     hb,
     ca,
@@ -147,6 +144,9 @@
     n_t,
     gn_t,
     e_t,
+    wout_f,
+    wn2_f,
+    both,
     send,
     recv,
 ):
@@ -334,66 +334,56 @@
         push("hs", hs_b, hs_g.at[d - 1], at_y(d))
     hand_on("wn2", wn2_g)
     geo = t_dot(ge, hidden)
-    wn2 = wn_ref[1]
     arrived("wout_c", wout_g.at[:, 1 - c])
+    arrived("wn2_c", wn2_g.at[:, 1 - c])
+    arrived("nb", nb_g)
+    wout_f[0:hs_w] = wout
+    wn2_f[:, 0:hs_w] = wn_ref[1]
+    for d in range(1, ny):
+        share = slice(d * hs_w, (d + 1) * hs_w)
+        wout_f[share] = wout_g[d - 1].reshape(hs_w, d_feat)
+        wn2_f[:, share] = wn2_g[d - 1].reshape(d_feat, hs_w)
+    both[...] = dot(wout_f[...], wn2_f[...]).astype(BF16)
+    before = jnp.concatenate(
+        [base_n] + [nb_g[d - 1, 1].astype(F32) for d in range(1, ny)], axis=1
+    )
+    gradient = jnp.concatenate(
+        [gn_w] + [nb_g[d - 1, 0].astype(F32) for d in range(1, ny)], axis=1
+    )
+
     arrived("hs", hs_g)
     for d in far_first(ny):
         yd = pl.multiple_of(lax.rem(y + d, ny) * fs_w + c * fw2, fw2)
         push("rows", win_ref.at[:, pl.ds(yd, fw2)], rows_g.at[d - 1, c], at_y(d))
         push("wn1", wn_ref.at[0, pl.ds(yd, fw2)], wn1_g.at[d - 1, c], at_y(d))
-    agg = dot(hs, wout)
-    for d in range(1, ny):
-        agg += dot(hs_g[d - 1], wout_g[d - 1].reshape(hs_w, d_feat))
-    agg = agg.astype(BF16)
-
-    arrived("wn2_c", wn2_g.at[:, 1 - c])
-    arrived("nb", nb_g)
-
-    def unit_grad(before, gradient, weight):
-        npre = before + dot(agg, weight)
-        nsg = sigmoid(npre)
-        slope = nsg * (1.0 + npre * (1.0 - nsg))
-        return npre * nsg, (gradient * slope).astype(BF16)
-
-    nhid, npg = unit_grad(base_n, gn_w, wn2)
-    nhid = nhid.astype(BF16)
-    npgs = [npg]
-    grad_agg = dot_t(npg, wn2)
-    for d in range(1, ny):
-        weight = wn2_g[d - 1].reshape(d_feat, hs_w)
-        _, other = unit_grad(
-            nb_g[d - 1, 1].astype(F32), nb_g[d - 1, 0].astype(F32), weight
-        )
-        npgs.append(other)
-        grad_agg += dot_t(other, weight)
-    grad_agg = grad_agg.astype(BF16)
+    hs_f = jnp.concatenate([hs] + [hs_g[d - 1] for d in range(1, ny)], axis=1)
+    npre = before + dot(hs_f, both[...])
+    nsg = sigmoid(npre)
+    nhid = (npre * nsg)[:, 0:hs_w].astype(BF16)
+    npg_f = (gradient * (nsg * (1.0 + npre * (1.0 - nsg)))).astype(BF16)
+    npgs = [npg_f[:, d * hs_w : (d + 1) * hs_w] for d in range(ny)]
+    npg = npgs[0]
+    agg = dot(hs_f, wout_f[...]).astype(BF16)
 
     ni, eo, ei = 2 * d_feat // owners, d_feat // owners, 3 * d_feat // owners
 
     def owner(n):
         return n % 2, (n // 2) % nx, n // nxc
 
-    def for_owners(blocks, sources, out):
+    def in_fours(start, size, value):
+        fours = value.reshape(-1, 4, hs_w).astype(BF16)
         for n in range(owners):
             oc, ox, oz = owner(n)
-            at, start = blocks.at[oc, ox, oz], 0
-            for size, source in sources:
-                if len(blocks.shape) == 5:
-                    at[start : start + size] = source[n * size : (n + 1) * size]
-                else:
-                    for row in range(0, size, 4):
-                        four = source[n * size + row : n * size + row + 4]
-                        at[(start + row) // 4] = four
-                start += size
-        out[...] = blocks[...].astype(BF16)
-
-    g4[...] = dot(gn_t[...], nhid)
-    g2[0:d_feat] = dot(n_t[...], npg)
-    g2[d_feat:] = t_dot(agg, npg)
-    for_owners(ga_f, ((ni, g2), (eo, g4)), ha)
+            for i in range(size // 4):
+                ha[oc, ox, oz, start // 4 + i] = fours[n * size // 4 + i]
+
+    in_fours(
+        0, ni, jnp.concatenate([dot(n_t[...], npg), t_dot(agg, npg)], axis=0)
+    )
+    in_fours(ni, eo, dot(gn_t[...], nhid))
     push("core_a", ha.at[1 - c], ca, {"c": 1 - c})
 
-    epg = ((ge_w + picked(hot_r[...], dot_t(grad_agg, wout))) * slope).astype(BF16)
+    epg = ((ge_w + picked(hot_r[...], dot_t(npg_f, both[0:hs_w]))) * slope).astype(BF16)
     epg_b[...] = epg
     for d in far_first(ny):
         push("epg", epg_b, epg_g.at[d - 1], at_y(d))
@@ -422,6 +412,7 @@
             total += got[d - 1].astype(F32)
         return total
 
+    grad_agg = dot_t(npg_f, wn2_f[...]).astype(BF16)
     s_sum = dot(hot_st, epg)
     s_hot = s_sum.astype(BF16)
     h_hot = dot(hot_ht, epg).astype(BF16)
@@ -432,7 +423,11 @@
     arrived("raw2", r2.at[pl.ds(1, nz - 1)])
     halo = r2[...].reshape(owners, d_feat)
     g1[d_feat : 2 * d_feat] = dot(n_t[...], s_hot) + t_dot(halo, h_hot)
-    for_owners(gb_f, ((ei, g1), (eo, g3)), hb)
+    for n in range(owners):
+        oc, ox, oz = owner(n)
+        gb_f[oc, ox, oz, 0:ei] = g1[n * ei : (n + 1) * ei]
+        gb_f[oc, ox, oz, ei:] = g3[n * eo : (n + 1) * eo]
+    hb[...] = gb_f[...].astype(BF16)
     push("core_b", hb.at[1 - c], cb, {"c": 1 - c})
     add_core("core_a", ha, ca, "x_a", xa, rxa)
 
@@ -573,11 +568,8 @@
             vm((ny - 1, nd, hw), BF16),
             vm((ed, hw), BF16),
             vm((ny - 1, ed, hw), BF16),
-            vm((2, nx, nz, ra, 4, hw), F32),
             vm((2, nx, nz, rb, hw), F32),
             vm((3 * d, hw), F32),
-            vm((2 * d, hw), F32),
-            vm((d, hw), F32),
             vm((d, hw), F32),
             vm((2, nx, nz, ra, 4, hw), BF16),
             vm((2, nx, nz, rb, hw), BF16),
@@ -600,6 +592,9 @@
             vm((d, nd), BF16),
             vm((d, nd), BF16),
             vm((d, ed), BF16),
+            vm((ny * hw, d), BF16),
+            vm((d, ny * hw), BF16),
+            vm((ny * hw, ny * hw), BF16),
             pltpu.SemaphoreType.DMA((phases,)),
             pltpu.SemaphoreType.DMA((phases,)),
         ],

time: 51.3 us -> 50.5 us (0.984)
  Pallas kernels: 50.6 us -> 49.7 us
    pallas_call x1, Pallas kernels: 49.9 us -> 49 us  [body(): pl.pallas_call(functools.partial(kernel, nz, nx, ny), out_shape=(vm((ed +...]
where the time goes in v5:
time: 50.5 us; the launch traced here: 50.3 us
  Pallas kernels  49.7 us (98%)
  between operations  0.65 us (1%)
    pallas_call x1, Pallas kernels, body(): pl.pallas_call(functools.partial(kernel, nz, nx, ny), out_shape=(vm((ed +...  49 us

profile of v5, /device:TPU:1, one launch (start us, length us, event | category | flops | bytes accessed | tf_op | source)
XLA Modules:
  0.0 50.3 jit_solution(9849078264995429267)
XLA Ops:
  0.6 49.0 %shard_map.181 = (bf16[512,128]{1,0:T(8,128)(2,1)S(1)}, f32[28,128]{1,0:T(8,128)S(1)}) custom-call(s32[1,128]{1,0:T(1,128)} %bitcast.9, s32[384]{0:T(512)} %snd_in.1, s32[384]{0:T(512)} %rcv_in.1, s32[3]{0:T(128)} %vc_in.1, bf16[128,512]{1,0:T(8,128)(2,1)} %n_in.1, bf16[384,512]{1,0:T(8,128)(2,1)} %e_in.1, bf16[128,512]{1,0:T(8,128)(2,1)} %gn_in.1, ...), custom_call_target="tpu_custom_call" | custom-call | tf_op jit(solution)/shard_map/pallas_call | solution.py:534
  49.7 0.7 %shard_map.182 = (bf16[128,128]{1,0:T(8,128)(2,1)}, bf16[384,128]{1,0:T(8,128)(2,1)}, f32[12,128]{1,0:T(8,128)}, f32[4,128]{1,0:T(4,128)}, f32[8,128]{1,0:T(8,128)}, /*index=5*/f32[4,128]{1,0:T(4,128)}) custom-call(bf16[512,128]{1,0:T(8,128)(2,1)S(1)} %get-tuple-element.14.wide, f32[28,128]{1,0:T(8,128)S(1)} %get-tuple-element.15.rows), custom_call_target="tpu_custom_call" | custom-call | tf_op jit(solution)/shard_map/pallas_call | solution.py:618

commit v6 on v5

--- a/solution.py
+++ b/solution.py
@@ -236,37 +236,39 @@
         out1[k] = rows_out[k * nz : (k + 1) * nz]
     r1[0] = rows_out[0:nz]
 
-    with jax.named_scope("entry"):
-        pl.semaphore_wait(barrier, len(peers))
-
-    for k, d in everyone:
-        push("halo", p_out.at[k * nz + d], p_in.at[k * nz + d], at_xc(k) | at_z(d))
-    for k in range(1, nxc):
-        push("raw1", out1.at[k], r1.at[k], at_xc(k))
-
-    hw2, dw2, fw2 = hs_w // 2, d_feat // 2, fs_w // 2
-    for copy in loads[3:5]:
-        copy.wait()
-    for d in far_first(ny):
-        push("wout", wout_ref.at[pl.ds(c * hw2, hw2)], wout_g.at[d - 1, c], at_y(d))
-    for d in far_first(ny):
-        push("wn2", wn_ref.at[1, pl.ds(c * dw2, dw2)], wn2_g.at[d - 1, c], at_y(d))
-
-    def hand_on(phase, buf):
-        arrived(phase, buf.at[:, c])
-        for d in far_first(ny):
-            push(phase + "_c", buf.at[d - 1, c], buf.at[d - 1, c], {"c": 1 - c})
-
-    for copy in loads[5:]:
-        copy.wait()
+    early = (3, 4, 10, 12, 13)
+    for i in early:
+        loads[i].wait()
     gn = gn_ref[...]
     gn_w = dot_t(gn, wno_ref[...])
     base_n = dot(nodes, wn_ref[0]) + bn_ref[...]
     nb_b[0] = gn_w.astype(BF16)
     nb_b[1] = base_n.astype(BF16)
+
+    with jax.named_scope("entry"):
+        pl.semaphore_wait(barrier, len(peers))
+
+    hw2, dw2, fw2 = hs_w // 2, d_feat // 2, fs_w // 2
+    for d in far_first(ny):
+        push("wout", wout_ref.at[pl.ds(c * hw2, hw2)], wout_g.at[d - 1, c], at_y(d))
+    for d in far_first(ny):
+        push("wn2", wn_ref.at[1, pl.ds(c * dw2, dw2)], wn2_g.at[d - 1, c], at_y(d))
     for d in far_first(ny):
         push("nb", nb_b, nb_g.at[d - 1], at_y(d))
 
+    for k, d in everyone:
+        push("halo", p_out.at[k * nz + d], p_in.at[k * nz + d], at_xc(k) | at_z(d))
+    for k in range(1, nxc):
+        push("raw1", out1.at[k], r1.at[k], at_xc(k))
+
+    def hand_on(phase, buf):
+        arrived(phase, buf.at[:, c])
+        for d in far_first(ny):
+            push(phase + "_c", buf.at[d - 1, c], buf.at[d - 1, c], {"c": 1 - c})
+
+    for i in range(5, len(loads)):
+        if i not in early:
+            loads[i].wait()
     snd, rcv = snd_ref[...].reshape(1, ed), rcv_ref[...].reshape(1, ed)
 
     def remote(k, dz):
@@ -284,11 +286,13 @@
     hot_rt = hot(iota((nd, ed), 0) == rcv)
 
     def picked(onehot, table):
-        high, low = two_parts(table)
-        return dot(onehot, high) + dot(onehot, low)
-
-    hot_p[...] = jnp.transpose(hot_pt)
-    hot_r[...] = jnp.transpose(hot_rt)
+        return dot(onehot, jnp.concatenate(two_parts(table), axis=0))
+
+    def twice(onehot_t):
+        return jnp.concatenate([jnp.transpose(onehot_t)] * 2, axis=1)
+
+    hot_p[...] = twice(hot_pt)
+    hot_r[...] = twice(hot_rt)
 
     live = jnp.concatenate(
         [
@@ -301,7 +305,7 @@
     base = (
         dot(edges, win_ref[0])
         + be_ref[...]
-        + picked(jnp.transpose(hot_st), dot(nodes, win_ref[1]))
+        + picked(twice(hot_st), dot(nodes, win_ref[1]))
         + picked(hot_r[...], dot(nodes, win_ref[2]))
     )
     ge = ge_ref[...]
@@ -420,6 +424,7 @@
     g3[...] = geo + t_dot(grad_agg, hs)
     g1[0:d_feat] = dot(e_t[...], epg)
     g1[2 * d_feat :] = dot(n_t[...], r_hot)
+    add_core("core_a", ha, ca, "x_a", xa, rxa)
     arrived("raw2", r2.at[pl.ds(1, nz - 1)])
     halo = r2[...].reshape(owners, d_feat)
     g1[d_feat : 2 * d_feat] = dot(n_t[...], s_hot) + t_dot(halo, h_hot)
@@ -429,7 +434,6 @@
         gb_f[oc, ox, oz, ei:] = g3[n * eo : (n + 1) * eo]
     hb[...] = gb_f[...].astype(BF16)
     push("core_b", hb.at[1 - c], cb, {"c": 1 - c})
-    add_core("core_a", ha, ca, "x_a", xa, rxa)
 
     back_out[...] = dot(hot_pt, epg).reshape(owners, 1, hs_w)
     back_in[0] = back_out[0]
@@ -587,8 +591,8 @@
             vm((owners, 1, hw), F32),
             vm((nd, hw), BF16),
             vm((ny - 1, nd, hw), BF16),
-            vm((ed, owners), BF16),
-            vm((ed, nd), BF16),
+            vm((ed, 2 * owners), BF16),
+            vm((ed, 2 * nd), BF16),
             vm((d, nd), BF16),
             vm((d, nd), BF16),
             vm((d, ed), BF16),

time: 50.5 us -> 51 us (level)
    pallas_call x1, Pallas kernels: 49 us -> 49.5 us  [body(): pl.pallas_call(functools.partial(kernel, nz, nx, ny), out_shape=(vm((ed +...]
where the time goes in v6:
time: 51 us; the launch traced here: 50.9 us
  Pallas kernels  50.2 us (98%)
  between operations  0.65 us (1%)
    pallas_call x1, Pallas kernels, body(): pl.pallas_call(functools.partial(kernel, nz, nx, ny), out_shape=(vm((ed +...  49.5 us

profile of v6, /device:TPU:1, one launch (start us, length us, event | category | flops | bytes accessed | tf_op | source)
XLA Modules:
  0.0 50.9 jit_solution(6023470466018679889)
XLA Ops:
  0.6 49.5 %shard_map.181 = (bf16[512,128]{1,0:T(8,128)(2,1)S(1)}, f32[28,128]{1,0:T(8,128)S(1)}) custom-call(s32[1,128]{1,0:T(1,128)} %bitcast.9, s32[384]{0:T(512)} %snd_in.1, s32[384]{0:T(512)} %rcv_in.1, s32[3]{0:T(128)} %vc_in.1, bf16[128,512]{1,0:T(8,128)(2,1)} %n_in.1, bf16[384,512]{1,0:T(8,128)(2,1)} %e_in.1, bf16[128,512]{1,0:T(8,128)(2,1)} %gn_in.1, ...), custom_call_target="tpu_custom_call" | custom-call | tf_op jit(solution)/shard_map/pallas_call | solution.py:538
  50.2 0.7 %shard_map.182 = (bf16[128,128]{1,0:T(8,128)(2,1)}, bf16[384,128]{1,0:T(8,128)(2,1)}, f32[12,128]{1,0:T(8,128)}, f32[4,128]{1,0:T(4,128)}, f32[8,128]{1,0:T(8,128)}, /*index=5*/f32[4,128]{1,0:T(4,128)}) custom-call(bf16[512,128]{1,0:T(8,128)(2,1)S(1)} %get-tuple-element.14.wide, f32[28,128]{1,0:T(8,128)S(1)} %get-tuple-element.15.rows), custom_call_target="tpu_custom_call" | custom-call | tf_op jit(solution)/shard_map/pallas_call | solution.py:622

commit v7 on v5

--- a/solution.py
+++ b/solution.py
@@ -284,11 +284,13 @@
     hot_rt = hot(iota((nd, ed), 0) == rcv)
 
     def picked(onehot, table):
-        high, low = two_parts(table)
-        return dot(onehot, high) + dot(onehot, low)
-
-    hot_p[...] = jnp.transpose(hot_pt)
-    hot_r[...] = jnp.transpose(hot_rt)
+        return dot(onehot, jnp.concatenate(two_parts(table), axis=0))
+
+    def twice(onehot_t):
+        return jnp.concatenate([jnp.transpose(onehot_t)] * 2, axis=1)
+
+    hot_p[...] = twice(hot_pt)
+    hot_r[...] = twice(hot_rt)
 
     live = jnp.concatenate(
         [
@@ -301,7 +303,7 @@
     base = (
         dot(edges, win_ref[0])
         + be_ref[...]
-        + picked(jnp.transpose(hot_st), dot(nodes, win_ref[1]))
+        + picked(twice(hot_st), dot(nodes, win_ref[1]))
         + picked(hot_r[...], dot(nodes, win_ref[2]))
     )
     ge = ge_ref[...]
@@ -587,8 +589,8 @@
             vm((owners, 1, hw), F32),
             vm((nd, hw), BF16),
             vm((ny - 1, nd, hw), BF16),
-            vm((ed, owners), BF16),
-            vm((ed, nd), BF16),
+            vm((ed, 2 * owners), BF16),
+            vm((ed, 2 * nd), BF16),
             vm((d, nd), BF16),
             vm((d, nd), BF16),
             vm((d, ed), BF16),

time: 50.5 us -> 50.8 us (level)
  no operation moved by 1% of the time
where the time goes in v7:
time: 50.8 us; the launch traced here: 50.7 us
  Pallas kernels  50 us (98%)
  between operations  0.65 us (1%)
    pallas_call x1, Pallas kernels, body(): pl.pallas_call(functools.partial(kernel, nz, nx, ny), out_shape=(vm((ed +...  49.4 us

profile of v7, /device:TPU:1, one launch (start us, length us, event | category | flops | bytes accessed | tf_op | source)
XLA Modules:
  0.0 50.7 jit_solution(4869927976683477636)
XLA Ops:
  0.6 49.4 %shard_map.181 = (bf16[512,128]{1,0:T(8,128)(2,1)S(1)}, f32[28,128]{1,0:T(8,128)S(1)}) custom-call(s32[1,128]{1,0:T(1,128)} %bitcast.9, s32[384]{0:T(512)} %snd_in.1, s32[384]{0:T(512)} %rcv_in.1, s32[3]{0:T(128)} %vc_in.1, bf16[128,512]{1,0:T(8,128)(2,1)} %n_in.1, bf16[384,512]{1,0:T(8,128)(2,1)} %e_in.1, bf16[128,512]{1,0:T(8,128)(2,1)} %gn_in.1, ...), custom_call_target="tpu_custom_call" | custom-call | tf_op jit(solution)/shard_map/pallas_call | solution.py:536
  50.0 0.7 %shard_map.182 = (bf16[128,128]{1,0:T(8,128)(2,1)}, bf16[384,128]{1,0:T(8,128)(2,1)}, f32[12,128]{1,0:T(8,128)}, f32[4,128]{1,0:T(4,128)}, f32[8,128]{1,0:T(8,128)}, /*index=5*/f32[4,128]{1,0:T(4,128)}) custom-call(bf16[512,128]{1,0:T(8,128)(2,1)S(1)} %get-tuple-element.14.wide, f32[28,128]{1,0:T(8,128)S(1)} %get-tuple-element.15.rows), custom_call_target="tpu_custom_call" | custom-call | tf_op jit(solution)/shard_map/pallas_call | solution.py:620
